TPU v7x, 32 devices: a whole 2x2x4 slice. The times are simulated.
32 devices in a mesh: cosmo: 2 (over y), shell: 4 (over x, core), band: 4 (over z).
Axes of the slice: x: 2, y: 2, z: 4, core: 2. Of those that a mesh axis runs over, the one named last changes fastest.
Arguments:
- cycle_modes: float32 [1024, 16, 2, 16], P(('cosmo', 'shell'), 'band'), parts along dimension 0, may hold values from -6 to 6
- cycle_weight: float32 [16], P('band'), may hold values from 0.5 to 2
- legendre: float32 [16, 16, 4096], P('band'), may hold values from -1.5 to 1.5
- spin_plus: bfloat16 [16, 16, 4096], P('band'), may hold values from -1.5 to 1.5
- spin_minus: bfloat16 [16, 16, 4096], P('band'), may hold values from -1.5 to 1.5
- window: float32 [512, 4096], P('shell'), may hold values from 0.3 to 3
- lensing: float32 [1024], P(('cosmo', 'shell')), parts along dimension 0, may hold values from 0.05 to 0.5
- source_shell: int32 [8], P('cosmo'), parts along dimension 0, may hold values from 384 to 511
Outputs:
- lensing_maps: float32 [8, 3, 16, 2, 16], P(('cosmo', 'shell'), None, 'band'), parts along dimension 0
There are 2 independent parts, one for each index of `cosmo`. A program takes and returns all parts, laid end to end along the dimension named above; an argument that names none is the same for every part. Nothing has to cross between parts.
All inputs are finite; a program needn't handle non-finite values.
Results may differ from a plain program's by a relative error of at most 0.00073.
Values sent between devices are 32-bit elements; how exact they have to be, the bound alone decides.
No kernel may reach another device: no remote copies, remote signals or barrier semaphores. Data moves between devices by JAX's collectives and lax.ppermute only.
A program may use at most 64 MiB of HBM per device.

v0:
```python
import jax
import jax.numpy as jnp
from jax import lax
from jax.sharding import PartitionSpec as P


def on_device(
    cycle_modes, cycle_weight, legendre, spin_plus, spin_minus, window, lensing, source_shell
):
    highest = lax.Precision.HIGHEST
    weighted = cycle_modes * cycle_weight[None, :, None, None]
    harmonic = jnp.einsum(
        "nrcm,mrl->nmcl",
        lax.all_to_all(weighted, "band", split_axis=3, concat_axis=1, tiled=True),
        legendre,
        precision=highest,
        preferred_element_type=jnp.float32,
    )
    local_shells = window.shape[0]
    degrees = legendre.shape[2]
    degree = jnp.arange(degrees).astype(jnp.float32)
    shell_ids = lax.axis_index("shell") * local_shells + jnp.arange(local_shells)
    efficiency = (
        lensing[None, :]
        * jnp.maximum(source_shell[:, None] - shell_ids[None, :], 0).astype(jnp.float32)
        / (source_shell[:, None] + 1).astype(jnp.float32)
    )
    binned = jnp.einsum(
        "bs,smcl->bmcl", efficiency, harmonic * window[:, None, None, :], precision=highest
    )
    shear_ratio = jnp.where(
        degree >= 2.0,
        jnp.sqrt((degree + 2.0) * (degree - 1.0) / jnp.maximum(degree * (degree + 1.0), 1.0)),
        0.0,
    )
    shear_coef = (-shear_ratio[None, None, None, :] * binned).astype(jnp.bfloat16)
    kappa_map = jnp.einsum(
        "bmcl,mrl->brcm", binned, legendre, precision=highest, preferred_element_type=jnp.float32
    )
    plus_map = jnp.einsum(
        "bmcl,mrl->brcm", shear_coef, spin_plus, preferred_element_type=jnp.float32
    )
    minus_map = jnp.einsum(
        "bmcl,mrl->brcm", shear_coef, spin_minus, preferred_element_type=jnp.float32
    )
    rotated = jnp.stack([-minus_map[:, :, 1], minus_map[:, :, 0]], axis=2)
    fields = jnp.stack([kappa_map, plus_map, rotated], axis=1)
    owned = lax.psum_scatter(fields, "shell", scatter_dimension=0, tiled=True)
    return lax.all_to_all(owned, "band", split_axis=2, concat_axis=4, tiled=True)


def solution(mesh):
    placed = (
        P(("cosmo", "shell"), "band", None, None),
        P("band"),
        P("band", None, None),
        P("band", None, None),
        P("band", None, None),
        P("shell", None),
        P(("cosmo", "shell")),
        P("cosmo"),
    )
    return jax.shard_map(
        on_device,
        mesh=mesh,
        in_specs=placed,
        out_specs=P(("cosmo", "shell"), None, "band", None, None),
        check_vma=False,
    )
```

profile of v0, /device:TPU:0, one launch (start us, length us, event | category | flops | bytes accessed | tf_op | source)
XLA Modules:
  0.0 58.7 jit_solution(11724573515361769660)
XLA Ops:
  0.0 0.0 copy-start
  0.0 1.1 %broadcast_multiply_fusion = f32[128,4,2,16]{0,3,2,1:T(8,128)S(1)} fusion(f32[128,4,2,16]{0,3,2,1:T(8,128)} %param.8, f32[4]{0:T(128)} %param.9), kind=kLoop, calls=%fused_computation.16 | loop fusion | flops 16384 | bytes 131088 | tf_op jit(solution)/shard_map/mul | solution.py:11
  1.1 0.7 %copy.38 = f32[128,4,2,16]{0,1,2,3:T(4,128)} copy(f32[128,4,2,16]{0,3,2,1:T(8,128)S(1)} %broadcast_multiply_fusion) | data formatting | bytes 131072 | tf_op jit(solution)/shard_map/mul | solution.py:11
  1.8 6.4 %all-to-all-start = ((f32[128,4,2,16]{0,1,2,3:T(4,128)}), f32[128,4,2,16]{0,1,2,3:T(4,128)S(1)}, u32[]{:S(2)}, u32[]{:S(2)}) async-start(f32[128,4,2,16]{0,1,2,3:T(4,128)} %copy.38), calls=%async_computation | async-start | bytes 131072 | tf_op jit(solution)/shard_map/all_to_all | solution.py:14
  8.1 0.7 %add_convert_fusion = f32[4]{0:T(128)S(1)} fusion(s32[4]{0:T(128)} %param.15), kind=kLoop, calls=%fused_computation.38 | loop fusion | flops 8 | bytes 32 | tf_op jit(solution)/shard_map/convert_element_type | solution.py:26
  8.8 1.2 %dynamic-slice = u32[1]{0:T(128)} dynamic-slice(u32[32]{0:T(128)} %constant.21, u32[]{:T(128)S(6)} %add.41), dynamic_slice_sizes={1} | dynamic-slice | bytes 12
  10.0 3.8 %all-to-all-done = f32[128,4,2,16]{0,1,2,3:T(4,128)S(1)} async-done(((f32[128,4,2,16]{0,1,2,3:T(4,128)}), f32[128,4,2,16]{0,1,2,3:T(4,128)S(1)}, u32[]{:S(2)}, u32[]{:S(2)}) %all-to-all-start) | async-done | bytes 65568 | tf_op jit(solution)/shard_map/all_to_all | solution.py:14
  13.9 0.0 copy-done
  13.9 13.5 %fusion.5 = f32[4,128,2,4096]{3,1,2,0:T(8,128)S(1)} fusion(f32[4,16,4096]{2,1,0:T(8,128)S(1)} %copy-done, f32[128,16,2,4]{0,1,3,2:T(8,128)S(1)} %bitcast.48), kind=kOutput, calls=%fused_computation.8 | convolution fusion | flops 805306368 | bytes 17891328 | tf_op jit(solution)/shard_map/nrcm,mrl->nmcl/dot_general | solution.py:12
  27.4 0.0 copy-done.4
  27.4 0.0 copy-done.1
  27.4 0.0 copy-done.5
  27.4 0.0 copy-start.2
  27.4 0.0 copy-start.3
  27.4 8.9 %fusion = f32[4,4,2,4096]{3,0,2,1:T(4,128)S(1)} fusion(f32[4,128,2,4096]{3,1,2,0:T(8,128)S(1)} %fusion.5, f32[128,4096]{1,0:T(8,128)S(1)} %copy-done.1, f32[4]{0:T(128)S(1)} %add_convert_fusion, s32[128]{0:T(128)S(1)} %iota_add_fusion, s32[4]{0:T(128)S(1)} %copy-done.4, f32[128]{0:T(128)S(1)} %copy-done.5), kind=kOutput, calls=%fused_computation | convolution fusion | flops 205523456 | bytes 19399712 | tf_op jit(solution)/shard_map/bs,smcl->bmcl/dot_general | solution.py:28
  36.3 1.4 %convolution_bitcast_fusion = f32[4,1,16,2,4]{2,0,3,4,1:T(4,128)S(1)} fusion(f32[4,4,2,4096]{3,0,2,1:T(4,128)S(1)} %fusion, f32[4,16,4096]{2,1,0:T(8,128)S(1)} %copy-done), kind=kOutput, calls=%fused_computation.4 | convolution fusion | flops 25165824 | bytes 1574912 | tf_op jit(solution)/shard_map/bmcl,mrl->brcm/dot_general | solution.py:37
  37.7 0.0 copy-done.2
  37.7 0.4 convolution_bitcast_fusion.1
  38.2 0.4 convolution_bitcast_fusion.2
  38.6 10.5 %all-reduce = f32[4,3,16,2,4]{2,4,3,1,0:T(4,128)S(1)} all-reduce(f32[4,3,16,2,4]{2,4,3,1,0:T(4,128)S(1)} %copy.41), channel_id=2, replica_groups=mesh['cosmo'=2,'shell'=4,'band'=4] {'shell'}, use_global_device_ids=true, to_apply=%region_0.1.clone | all-reduce | flops 1536 | bytes 12288
  49.2 0.7 %constant_dynamic-slice_fusion = f32[1,3,16,2,4]{2,4,3,1,0:T(4,128)S(1)} fusion(f32[4,3,16,2,4]{2,4,3,1,0:T(4,128)S(1)} %all-reduce, u32[]{:T(128)} %bitcast.28), kind=kLoop, calls=%fused_computation.37 | loop fusion | bytes 3076
  49.8 0.1 copy.42
  49.9 8.1 %all_to_all.36 = f32[1,3,16,2,4]{4,3,1,0,2:T(2,128)S(1)} all-to-all(f32[1,3,16,2,4]{4,3,1,0,2:T(2,128)S(1)} %copy.42), channel_id=1, replica_groups=mesh['cosmo'=2,'shell'=4,'band'=4] {'band'}, dimensions={2} | all-to-all | bytes 3072 | tf_op jit(solution)/shard_map/all_to_all | solution.py:49
  58.0 0.7 %all_to_all.33 = f32[1,3,4,2,16]{4,3,2,1,0:T(2,128)} reshape(f32[1,3,4,2,4,4]{5,4,3,2,1,0:T(4,128)S(1)} %bitcast.51) | data formatting | bytes 3072 | tf_op jit(solution)/shard_map/all_to_all | solution.py:49
  (12 shorter events, 0.1 us)
Async XLA Ops:
  0.0 13.9 %copy-start = (f32[4,16,4096]{2,1,0:T(8,128)S(1)}, f32[4,16,4096]{2,1,0:T(8,128)}, u32[]{:S(2)}) copy-start(f32[4,16,4096]{2,1,0:T(8,128)} %param.10) | copy-start | bytes 3145732
  0.0 27.4 %copy-start.4 = (s32[4]{0:T(128)S(1)}, s32[4]{0:T(128)}, u32[]{:S(2)}) copy-start(s32[4]{0:T(128)} %param.15) | copy-start | bytes 52
  0.0 27.4 %copy-start.1 = (f32[128,4096]{1,0:T(8,128)S(1)}, f32[128,4096]{1,0:T(8,128)}, u32[]{:S(2)}) copy-start(f32[128,4096]{1,0:T(8,128)} %param.13) | copy-start | bytes 6291460
  0.0 27.4 %copy-start.5 = (f32[128]{0:T(128)S(1)}, f32[128]{0:T(128)}, u32[]{:S(2)}) copy-start(f32[128]{0:T(128)} %param.14) | copy-start | bytes 1540
  1.8 12.1 %all-to-all-start = ((f32[128,4,2,16]{0,1,2,3:T(4,128)}), f32[128,4,2,16]{0,1,2,3:T(4,128)S(1)}, u32[]{:S(2)}, u32[]{:S(2)}) async-start(f32[128,4,2,16]{0,1,2,3:T(4,128)} %copy.38), calls=%async_computation | async-start | bytes 131072 | tf_op jit(solution)/shard_map/all_to_all | solution.py:14
  27.4 10.3 %copy-start.2 = (bf16[4,16,4096]{2,1,0:T(8,128)(2,1)S(1)}, bf16[4,16,4096]{2,1,0:T(8,128)(2,1)}, u32[]{:S(2)}) copy-start(bf16[4,16,4096]{2,1,0:T(8,128)(2,1)} %param.12) | copy-start | bytes 1572868
  27.4 10.8 %copy-start.3 = (bf16[4,16,4096]{2,1,0:T(8,128)(2,1)S(1)}, bf16[4,16,4096]{2,1,0:T(8,128)(2,1)}, u32[]{:S(2)}) copy-start(bf16[4,16,4096]{2,1,0:T(8,128)(2,1)} %param.11) | copy-start | bytes 1572868
where the time goes:
time: 59.1 us; the launch traced here: 58.7 us
  matrix products  24.6 us (42%)
  blocking collectives  18.6 us (31%)
  starting transfers between devices  6.35 us (11%)
  waiting for transfers between devices  3.8 us (6%)
  local copies, waits for them, and re-layouts  3.45 us (6%)
  other arithmetic  1.78 us (3%)
    dot_general x1, matrix products, on_device(): jnp.einsum('nrcm,mrl->nmcl', lax.all_to_all(weighted, 'band', split_axis=...  13.5 us
    unnamed x1, blocking collectives  10.5 us
    dot_general x1, matrix products, on_device(): jnp.einsum('bs,smcl->bmcl', efficiency, harmonic * window[:, None, None,...  8.91 us
    all_to_all x1, blocking collectives, on_device(): lax.all_to_all(owned, 'band', split_axis=2, concat_axis=4, tiled=True)  8.06 us
    all_to_all x1, starting transfers between devices, on_device(): lax.all_to_all(weighted, 'band', split_axis=3, concat_axis=1, tiled=True)  6.35 us
    all_to_all x1, waiting for transfers between devices, on_device(): lax.all_to_all(weighted, 'band', split_axis=3, concat_axis=1, tiled=True)  3.8 us
    unnamed x14, local copies, waits for them, and re-layouts  1.92 us
    dot_general x1, matrix products, on_device(): jnp.einsum('bmcl,mrl->brcm', binned, legendre, precision=highest, preferr...  1.39 us
  transfers between devices with their start and end apart: 1, of which 1 were waited for; matrix products, arithmetic and copies ran while one was open for 3% of the time, Pallas kernels for 0%

commit v1 on v0

v1 whole, which is shorter than its diff:
```python
import functools

import jax
import jax.numpy as jnp
from jax import lax
from jax.experimental import pallas as pl
from jax.experimental.pallas import tpu as pltpu
from jax.sharding import PartitionSpec as P

TILE = 256


def split(x):
    high = x.astype(jnp.bfloat16)
    low = (x - high.astype(jnp.float32)).astype(jnp.bfloat16)
    return high, low


def maps_kernel(
    first_shell_ref, source_ref, modes_ref, legendre_ref, plus_ref, minus_ref, window_ref, lensing_ref,
    out_ref, left_ref, sums_ref, *, bins, orders, cycles, degrees,
):
    shells = window_ref.shape[0]
    rows = 2 * bins
    sub = lax.broadcasted_iota(jnp.int32, (rows, shells), 0)
    shell_ids = first_shell_ref[0] + lax.broadcasted_iota(jnp.int32, (rows, shells), 1)
    source = jnp.zeros((rows, shells), jnp.int32)
    for b in range(bins):
        source = jnp.where(sub % bins == b, source_ref[b], source)
    efficiency = (
        lensing_ref[...]
        * jnp.maximum(source - shell_ids, 0).astype(jnp.float32)
        / (source + 1).astype(jnp.float32)
    )
    first_part = (sub < bins)[None]
    for m in range(orders):
        real = jnp.broadcast_to(modes_ref[:, m : m + 1, :], (cycles, rows, shells))
        imag = jnp.broadcast_to(modes_ref[:, orders + m : orders + m + 1, :], (cycles, rows, shells))
        left = (jnp.where(first_part, real, imag) * efficiency[None]).reshape(cycles * rows, shells)
        high, low = split(left)
        span = pl.ds(m * cycles * rows, cycles * rows)
        left_ref[span, 0:shells] = high
        left_ref[span, shells : 2 * shells] = low
        left_ref[span, 2 * shells : 3 * shells] = high

    def step(start, sums):
        lanes = pl.ds(start, TILE)
        high, low = split(window_ref[:, lanes])
        product = jnp.dot(
            left_ref[...], jnp.concatenate([high, high, low], 0), preferred_element_type=jnp.float32
        )
        parts = []
        for m in range(orders):
            binned = jnp.zeros((rows, TILE), jnp.float32)
            for r in range(cycles):
                at = (m * cycles + r) * rows
                binned = binned + legendre_ref[m, r : r + 1, lanes] * product[at : at + rows]
            parts.append(binned)
        binned = jnp.concatenate(parts, 0)
        degree = (start + lax.broadcasted_iota(jnp.int32, (rows, TILE), 1)).astype(jnp.float32)
        ratio = jnp.where(
            degree >= 2.0,
            jnp.sqrt((degree + 2.0) * (degree - 1.0) / jnp.maximum(degree * (degree + 1.0), 1.0)),
            0.0,
        )
        ratio = jnp.concatenate([ratio] * orders, 0)
        shear = (-ratio * binned).astype(jnp.bfloat16)
        high, low = split(binned)
        table_high, table_low = split(legendre_ref[:, :, lanes].reshape(orders * cycles, TILE))
        tables = jnp.concatenate(
            [
                table_high,
                table_low,
                plus_ref[:, :, lanes].reshape(orders * cycles, TILE),
                minus_ref[:, :, lanes].reshape(orders * cycles, TILE),
            ],
            0,
        )
        return sums + lax.dot_general(
            jnp.concatenate([high, low, shear], 0),
            tables,
            (((1,), (1,)), ((), ())),
            preferred_element_type=jnp.float32,
        )

    columns = orders * cycles
    sums = jnp.zeros((3 * orders * rows, 4 * columns), jnp.float32)
    if cycles * orders <= 64:
        for start in range(0, degrees, TILE):
            sums = step(start, sums)
        sums_ref[...] = sums
    else:
        sums_ref[...] = sums

        @pl.loop(0, degrees // TILE)
        def _(i):
            sums_ref[...] = step(pl.multiple_of(i * TILE, TILE), sums_ref[...])

    lane = lax.broadcasted_iota(jnp.int32, (rows, columns), 1)

    def own(kind, table):
        total = jnp.zeros((rows, columns), jnp.float32)
        for m in range(orders):
            block = sums_ref[pl.ds((kind * orders + m) * rows, rows), table * columns : (table + 1) * columns]
            total = jnp.where(lane // cycles == m, block, total)
        return total

    out_ref[0] = own(0, 0) + own(0, 1) + own(1, 0)
    out_ref[1] = own(2, 2)
    minus = own(2, 3)
    turned = jnp.concatenate([-minus[bins:], minus[:bins]], 0)
    out_ref[2] = turned


def on_device(
    cycle_modes, cycle_weight, legendre, spin_plus, spin_minus, window, lensing, source_shell
):
    bands = lax.axis_size("band")
    shell_parts = lax.axis_size("shell")
    shells, cycles_here, _, orders_all = cycle_modes.shape
    orders, cycles, degrees = legendre.shape
    bins = source_shell.shape[0]
    own_bins = bins // shell_parts
    weighted = cycle_modes.transpose(1, 2, 3, 0) * cycle_weight[:, None, None, None]
    weighted = weighted.reshape(cycles_here, 2, bands, orders, shells).transpose(2, 0, 1, 3, 4)
    weighted = weighted.reshape(bands, cycles_here, 2 * orders, shells)
    modes = lax.all_to_all(weighted, "band", split_axis=0, concat_axis=0, tiled=True)
    modes = modes.reshape(cycles, 2 * orders, shells)
    first_shell = (lax.axis_index("shell") * shells).astype(jnp.int32).reshape(1)
    smem = pl.BlockSpec(memory_space=pltpu.SMEM)
    vmem = pl.BlockSpec(memory_space=pltpu.VMEM)
    maps = pl.pallas_call(
        functools.partial(maps_kernel, bins=bins, orders=orders, cycles=cycles, degrees=degrees),
        in_specs=[smem, smem] + [vmem] * 6,
        out_specs=vmem,
        out_shape=jax.ShapeDtypeStruct((3, 2 * bins, orders * cycles), jnp.float32),
        scratch_shapes=[
            pltpu.VMEM((orders * cycles * 2 * bins, 3 * shells), jnp.bfloat16),
            pltpu.VMEM((3 * orders * 2 * bins, 4 * orders * cycles), jnp.float32),
        ],
        compiler_params=pltpu.CompilerParams(vmem_limit_bytes=24 * 2**20),
        name="maps",
    )(first_shell, source_shell, modes, legendre, spin_plus, spin_minus, window, lensing.reshape(1, shells))
    maps = maps.reshape(3, 2, shell_parts, own_bins, orders, bands, cycles_here).transpose(2, 5, 3, 0, 6, 1, 4)
    block = own_bins * 3 * cycles_here * 2 * orders
    maps = maps.reshape(shell_parts * bands, block)
    got = lax.all_to_all(maps, ("shell", "band"), split_axis=0, concat_axis=0, tiled=True)
    got = got.reshape(shell_parts, bands, own_bins, 3, cycles_here, 2, orders).sum(0)
    return got.transpose(1, 2, 3, 4, 0, 5).reshape(own_bins, 3, cycles_here, 2, orders_all)


def solution(mesh):
    placed = (
        P(("cosmo", "shell"), "band", None, None),
        P("band"),
        P("band", None, None),
        P("band", None, None),
        P("band", None, None),
        P("shell", None),
        P(("cosmo", "shell")),
        P("cosmo"),
    )
    return jax.shard_map(
        on_device,
        mesh=mesh,
        in_specs=placed,
        out_specs=P(("cosmo", "shell"), None, "band", None, None),
        check_vma=False,
    )
```

time: 59.1 us -> 37.7 us (0.64)
  matrix products: 24.6 us -> 0 us
  blocking collectives: 18.6 us -> 9.41 us
  local copies, waits for them, and re-layouts: 3.45 us -> 9.54 us
  Pallas kernels: 0 us -> 4.45 us
  waiting for transfers between devices: 3.8 us -> 5.74 us
    dot_general x5 -> x0, matrix products: 24.6 us -> none  [the longest x1 13.5 us: on_device(): jnp.einsum('nrcm,mrl->nmcl', lax.all_to_all(weighted, 'band', split_axis=...]
    unnamed x1 -> x0, blocking collectives: 10.5 us -> none
    pallas_call x0 -> x1, Pallas kernels: none -> 4.45 us  [on_device(): pl.pallas_call(functools.partial(maps_kernel, bins=bins, orders=orders, c...]
    unnamed x14 -> x12, local copies, waits for them, and re-layouts: 1.92 us -> 6.21 us
    reshape x0 -> x4, local copies, waits for them, and re-layouts: none -> 1.95 us  [the longest x2 0.96 us: on_device(): maps.reshape(3, 2, shell_parts, own_bins, orders, bands, cycles_here)]
    all_to_all x1, waiting for transfers between devices: 3.8 us -> 5.74 us  [on_device(): lax.all_to_all(weighted, 'band', split_axis=0, concat_axis=0, tiled=True)]
    all_to_all x1, blocking collectives: 8.06 us -> 9.41 us  [on_device(): lax.all_to_all(maps, ('shell', 'band'), split_axis=0, concat_axis=0, tile...]
    mul x1 -> x0, local copies, waits for them, and re-layouts: 0.67 us -> none  [on_device(): weighted = cycle_modes * cycle_weight[None, :, None, None]]
  transfers between devices with their start and end apart: 1 -> 1, of which waited for: 1 -> 1; matrix products, arithmetic and copies ran while one was open for 3% -> 0% of each run, Pallas kernels for 0% -> 0%
where the time goes in v1:
time: 37.7 us; the launch traced here: 37.2 us
  local copies, waits for them, and re-layouts  9.54 us (25%)
  blocking collectives  9.41 us (25%)
  starting transfers between devices  6.35 us (17%)
  waiting for transfers between devices  5.74 us (15%)
  Pallas kernels  4.45 us (12%)
  other arithmetic  1.69 us (4%)
    all_to_all x1, blocking collectives, on_device(): lax.all_to_all(maps, ('shell', 'band'), split_axis=0, concat_axis=0, tile...  9.41 us
    all_to_all x1, starting transfers between devices, on_device(): lax.all_to_all(weighted, 'band', split_axis=0, concat_axis=0, tiled=True)  6.35 us
    unnamed x12, local copies, waits for them, and re-layouts  6.21 us
    all_to_all x1, waiting for transfers between devices, on_device(): lax.all_to_all(weighted, 'band', split_axis=0, concat_axis=0, tiled=True)  5.74 us
    pallas_call x1, Pallas kernels, on_device(): pl.pallas_call(functools.partial(maps_kernel, bins=bins, orders=orders, c...  4.45 us
    reshape x2, local copies, waits for them, and re-layouts, on_device(): maps.reshape(3, 2, shell_parts, own_bins, orders, bands, cycles_here)  0.96 us
    mul x1, other arithmetic, on_device(): cycle_modes.transpose(1, 2, 3, 0) * cycle_weight[:, None, None, None]  0.91 us
  transfers between devices with their start and end apart: 1, of which 1 were waited for; matrix products, arithmetic and copies ran while one was open for 0% of the time, Pallas kernels for 0%

profile of v1, /device:TPU:0, one launch (start us, length us, event | category | flops | bytes accessed | tf_op | source)
XLA Modules:
  0.0 37.2 jit_solution(16491435093575790770)
XLA Ops:
  0.0 0.9 %broadcast_multiply_fusion = f32[128,4,2,16]{0,3,2,1:T(8,128)S(1)} fusion(f32[128,4,2,16]{0,3,2,1:T(8,128)} %param.8, f32[4]{0:T(128)} %param.9), kind=kLoop, calls=%fused_computation | loop fusion | flops 16384 | bytes 131088 | tf_op jit(solution)/shard_map/mul | solution.py:124
  0.9 0.6 %copy.15 = f32[4,4,2,4,128]{4,3,2,1,0:T(4,128)} copy(f32[4,4,2,4,128]{4,3,0,2,1:T(4,128)S(1)} %bitcast.19) | data formatting | bytes 131072 | tf_op jit(solution)/shard_map/transpose | solution.py:125
  1.5 6.3 %all-to-all-start = ((f32[4,4,8,128]{3,2,1,0:T(8,128)}), f32[4,4,8,128]{3,2,1,0:T(8,128)S(1)}, u32[]{:S(2)}, u32[]{:S(2)}) async-start(f32[4,4,8,128]{3,2,1,0:T(8,128)} %bitcast.4), calls=%async_computation | async-start | bytes 131072 | tf_op jit(solution)/shard_map/all_to_all | solution.py:127
  7.9 5.7 %all-to-all-done = f32[4,4,8,128]{3,2,1,0:T(8,128)S(1)} async-done(((f32[4,4,8,128]{3,2,1,0:T(8,128)}), f32[4,4,8,128]{3,2,1,0:T(8,128)S(1)}, u32[]{:S(2)}, u32[]{:S(2)}) %all-to-all-start) | async-done | bytes 65568 | tf_op jit(solution)/shard_map/all_to_all | solution.py:127
  13.6 0.0 copy-start
  13.6 1.6 %copy-done = f32[128,4096]{1,0:T(8,128)S(1)} copy-done((f32[128,4096]{1,0:T(8,128)S(1)}, f32[128,4096]{1,0:T(8,128)}, u32[]{:S(2)}) %copy-start) | copy-done | bytes 2097176
  15.2 0.0 copy-start.1
  15.2 1.2 %copy-done.1 = f32[4,16,4096]{2,1,0:T(8,128)S(1)} copy-done((f32[4,16,4096]{2,1,0:T(8,128)S(1)}, f32[4,16,4096]{2,1,0:T(8,128)}, u32[]{:S(2)}) %copy-start.1) | copy-done | bytes 1048600
  16.5 0.0 copy-start.2
  16.5 1.0 %copy-done.2 = bf16[4,16,4096]{2,1,0:T(8,128)(2,1)S(1)} copy-done((bf16[4,16,4096]{2,1,0:T(8,128)(2,1)S(1)}, bf16[4,16,4096]{2,1,0:T(8,128)(2,1)}, u32[]{:S(2)}) %copy-start.2) | copy-done | bytes 524312
  17.5 1.0 %copy-done.3 = bf16[4,16,4096]{2,1,0:T(8,128)(2,1)S(1)} copy-done((bf16[4,16,4096]{2,1,0:T(8,128)(2,1)S(1)}, bf16[4,16,4096]{2,1,0:T(8,128)(2,1)}, u32[]{:S(2)}) %copy-start.3) | copy-done | bytes 524312
  18.5 0.0 copy-start.4
  18.5 0.7 %copy-done.4 = s32[4]{0:T(128)S(1)} copy-done((s32[4]{0:T(128)S(1)}, s32[4]{0:T(128)}, u32[]{:S(2)}) %copy-start.4) | copy-done | bytes 40
  19.2 0.7 %copy-done.5 = f32[128]{0:T(128)S(1)} copy-done((f32[128]{0:T(128)S(1)}, f32[128]{0:T(128)}, u32[]{:S(2)}) %copy-start.5) | copy-done | bytes 536
  19.8 4.4 %maps.1 = f32[3,8,64]{2,1,0:T(8,128)S(1)} custom-call(s32[1]{0:T(128)} %bitcast.first_shell_ref, s32[4]{0:T(128)S(1)} %copy-done.4, f32[16,8,128]{2,1,0:T(8,128)S(1)} %bitcast.16, f32[4,16,4096]{2,1,0:T(8,128)S(1)} %copy-done.1, bf16[4,16,4096]{2,1,0:T(8,128)(2,1)S(1)} %copy-done.2, bf16[4,16,4096]{2,1,0:T(8,128)(2,1)S(1)} %copy-done.3, ...), custom_call_target="tpu_custom_call" | custom-call | tf_op jit(solution)/shard_map/maps/pallas_call | solution.py:132
  24.3 0.3 reshape.36
  24.6 0.7 %copy.16 = f32[3,2,4,1,4,4,4]{4,1,6,0,5,2,3:T(2,128)S(1)} copy(f32[3,2,4,1,4,4,4]{6,5,4,2,1,0,3:T(4,128)S(1)} %reshape.36) | data formatting | bytes 12288 | tf_op jit(solution)/shard_map/reshape | solution.py:144
  25.3 0.2 all_to_all.10
  25.5 9.4 %all_to_all.14 = f32[16,1,96]{2,1,0:T(1,128)S(1)} all-to-all(f32[16,1,96]{2,1,0:T(1,128)S(1)} %bitcast.21), channel_id=1, replica_groups=mesh['cosmo'=2,'shell'=4,'band'=4] {'shell','band'}, dimensions={0} | all-to-all | bytes 12288 | tf_op jit(solution)/shard_map/all_to_all | solution.py:147
  34.9 0.5 %broadcast.5 = f32[]{:T(128)} broadcast(f32[]{:T(128)} %constant.12), dimensions={} | broadcast | bytes 8 | tf_op jit(solution)/shard_map/all_to_all | solution.py:147
  35.4 0.7 %reduce.4 = f32[16,96]{1,0:T(8,128)S(1)} reduce(f32[16,1,96]{2,1,0:T(1,128)S(1)} %all_to_all.14, f32[]{:T(128)} %broadcast.5), dimensions={1}, to_apply=%all_to_all.11.reduce_sub_computation.3 | reduce | bytes 12292 | tf_op jit(solution)/shard_map/all_to_all | solution.py:147
  36.1 0.3 reshape.37
  36.4 0.1 reduce_sum.11
  36.5 0.7 %reshape.38 = f32[1,3,4,2,16]{4,3,2,1,0:T(2,128)} reshape(f32[1,3,4,2,4,4]{5,4,3,2,1,0:T(4,128)S(1)} %copy.18) | data formatting | bytes 3072 | tf_op jit(solution)/shard_map/reshape | solution.py:149
  (3 shorter events, 0.0 us)
Async XLA Ops:
  1.5 12.1 %all-to-all-start = ((f32[4,4,8,128]{3,2,1,0:T(8,128)}), f32[4,4,8,128]{3,2,1,0:T(8,128)S(1)}, u32[]{:S(2)}, u32[]{:S(2)}) async-start(f32[4,4,8,128]{3,2,1,0:T(8,128)} %bitcast.4), calls=%async_computation | async-start | bytes 131072 | tf_op jit(solution)/shard_map/all_to_all | solution.py:127
  13.6 1.6 %copy-start = (f32[128,4096]{1,0:T(8,128)S(1)}, f32[128,4096]{1,0:T(8,128)}, u32[]{:S(2)}) copy-start(f32[128,4096]{1,0:T(8,128)} %window_ref.1) | copy-start | bytes 6291460
  15.2 1.2 %copy-start.1 = (f32[4,16,4096]{2,1,0:T(8,128)S(1)}, f32[4,16,4096]{2,1,0:T(8,128)}, u32[]{:S(2)}) copy-start(f32[4,16,4096]{2,1,0:T(8,128)} %legendre_ref.1) | copy-start | bytes 3145732
  16.5 1.0 %copy-start.2 = (bf16[4,16,4096]{2,1,0:T(8,128)(2,1)S(1)}, bf16[4,16,4096]{2,1,0:T(8,128)(2,1)}, u32[]{:S(2)}) copy-start(bf16[4,16,4096]{2,1,0:T(8,128)(2,1)} %plus_ref.1) | copy-start | bytes 1572868
  17.5 1.0 %copy-start.3 = (bf16[4,16,4096]{2,1,0:T(8,128)(2,1)S(1)}, bf16[4,16,4096]{2,1,0:T(8,128)(2,1)}, u32[]{:S(2)}) copy-start(bf16[4,16,4096]{2,1,0:T(8,128)(2,1)} %minus_ref.1) | copy-start | bytes 1572868
  18.5 0.7 %copy-start.4 = (s32[4]{0:T(128)S(1)}, s32[4]{0:T(128)}, u32[]{:S(2)}) copy-start(s32[4]{0:T(128)} %source_ref.1) | copy-start | bytes 52
  19.2 0.7 %copy-start.5 = (f32[128]{0:T(128)S(1)}, f32[128]{0:T(128)}, u32[]{:S(2)}) copy-start(f32[128]{0:T(128)} %param.14) | copy-start | bytes 1540

commit v2 on v1

v2 whole, which is shorter than its diff:
```python
import functools

import jax
import jax.numpy as jnp
from jax import lax
from jax.experimental import pallas as pl
from jax.experimental.pallas import tpu as pltpu
from jax.sharding import PartitionSpec as P

TILE = 512
VMEM = pl.BlockSpec(memory_space=pltpu.VMEM)
HBM = pl.BlockSpec(memory_space=pltpu.HBM)
PARAMS = pltpu.CompilerParams(vmem_limit_bytes=28 * 2**20)
KAPPA_HIGH, KAPPA_LOW, PLUS, MINUS = range(4)


def keep(x):
    return pltpu.with_memory_space_constraint(x, pltpu.HBM)


def split(x):
    high = x.astype(jnp.bfloat16)
    low = (x - high.astype(jnp.float32)).astype(jnp.bfloat16)
    return high, low


def iota(shape, axis):
    return lax.broadcasted_iota(jnp.int32, shape, axis)


def pack_kernel(modes_in, weight_in, *out_refs, bands, orders, by_offset):
    *out_refs, blocks_ref, modes_ref, weight_ref, sems = out_refs
    cycles_here, _, _, shells = modes_ref.shape
    copies = [
        pltpu.make_async_copy(modes_in, modes_ref, sems.at[0]),
        pltpu.make_async_copy(weight_in, weight_ref, sems.at[1]),
    ]
    for copy in copies:
        copy.start()
    for copy in copies:
        copy.wait()
    for r in range(cycles_here):
        weight = jnp.broadcast_to(weight_ref[0:1, r : r + 1], (orders, shells))
        for c in range(2):
            for z in range(bands):
                blocks_ref[z, r, c * orders : (c + 1) * orders, :] = (
                    modes_ref[r, c, z * orders : (z + 1) * orders, :] * weight
                )
    if by_offset:
        here = lax.axis_index("band")
        for k in range(bands):
            out_refs[k][...] = blocks_ref[here ^ k]
    else:
        out_refs[0][...] = blocks_ref[...]


def left_of(modes, efficiency, orders, bins):
    cycles, _, shells = modes.shape
    rows = 2 * bins
    first_part = (iota((1, rows, shells), 1) < bins)
    parts = []
    for m in range(orders):
        real = jnp.broadcast_to(modes[:, m : m + 1, :], (cycles, rows, shells))
        imag = jnp.broadcast_to(modes[:, orders + m : orders + m + 1, :], (cycles, rows, shells))
        left = jnp.where(first_part, real, imag) * efficiency[None]
        parts.append(left.reshape(cycles * rows, shells))
    high, low = split(jnp.concatenate(parts, 0))
    return jnp.concatenate([high, low], 1), high


def add_cycles(binned, left, left_high, high, low, legendre_ref, firsts, lanes, orders, rows):
    product = jnp.dot(left, jnp.concatenate([high, high], 0), preferred_element_type=jnp.float32)
    product = product + jnp.dot(left_high, low, preferred_element_type=jnp.float32)
    out = []
    at = 0
    for m in range(orders):
        total = binned[m]
        for first, count in firsts:
            for r in range(count):
                total = total + legendre_ref[m, pl.ds(first + r, 1), lanes] * product[at : at + rows]
                at += rows
        out.append(total)
    return out


def prepare_kernel(
    source_in, lensing_in, legendre_in, plus_in, minus_in, window_in, *refs,
    bins, orders, cycles, cycles_here, degrees, chunk, own,
):
    if own:
        own_ref, *refs = refs
    efficiency_ref, legendre_ref, high_ref, low_ref, tables_ref, binned_ref = refs[:6]
    window_ref, plus_ref, minus_ref, source_ref, lensing_ref, sems, small_sems = refs[6:]
    shells = window_ref.shape[0]
    rows = 2 * bins
    bands = cycles // cycles_here

    def copies(i):
        lanes = pl.ds(i * chunk, chunk)
        return [
            pltpu.make_async_copy(window_in.at[:, lanes], window_ref.at[:, lanes], sems.at[0, i]),
            pltpu.make_async_copy(legendre_in.at[:, :, lanes], legendre_ref.at[:, :, lanes], sems.at[1, i]),
            pltpu.make_async_copy(plus_in.at[:, :, lanes], plus_ref.at[:, :, lanes], sems.at[2, i]),
            pltpu.make_async_copy(minus_in.at[:, :, lanes], minus_ref.at[:, :, lanes], sems.at[3, i]),
        ]

    chunks = degrees // chunk
    small = [
        pltpu.make_async_copy(source_in, source_ref, small_sems.at[0]),
        pltpu.make_async_copy(lensing_in, lensing_ref, small_sems.at[1]),
    ]
    for copy in small:
        copy.start()
    for i in range(chunks):
        for copy in copies(i):
            copy.start()
    for copy in small:
        copy.wait()

    row_bin = iota((rows, shells), 0) % bins
    source = jnp.zeros((rows, shells), jnp.int32)
    for b in range(bins):
        source = jnp.where(row_bin == b, jnp.broadcast_to(source_ref[0:1, b : b + 1], (rows, shells)), source)
    shell_ids = lax.axis_index("shell") * shells + iota((rows, shells), 1)
    efficiency = (
        lensing_ref[...]
        * jnp.maximum(source - shell_ids, 0).astype(jnp.float32)
        / (source + 1).astype(jnp.float32)
    )
    efficiency_ref[...] = efficiency
    if own:
        left, left_high = left_of(own_ref[...], efficiency, orders, bins)
        first = lax.axis_index("band") * cycles_here

    for i in range(chunks):
        lanes = pl.ds(i * chunk, chunk)
        for copy in copies(i):
            copy.wait()
        high, low = split(window_ref[:, lanes])
        high_ref[:, lanes] = high
        low_ref[:, lanes] = low
        for z in range(bands):
            at = z * cycles_here

            def rows_of(ref):
                return jnp.concatenate(
                    [ref[m, :, lanes].astype(jnp.float32)[at : at + cycles_here] for m in range(orders)], 0
                )

            table_high, table_low = split(rows_of(legendre_ref))
            block = orders * cycles_here
            for table, value in (
                (KAPPA_HIGH, table_high),
                (KAPPA_LOW, table_low),
                (PLUS, rows_of(plus_ref).astype(jnp.bfloat16)),
                (MINUS, rows_of(minus_ref).astype(jnp.bfloat16)),
            ):
                tables_ref[pl.ds((z * 4 + table) * block, block), lanes] = value
        if own:
            zero = [jnp.zeros((rows, chunk), jnp.float32)] * orders
            binned = add_cycles(
                zero, left, left_high, high, low, legendre_ref, [(first, cycles_here)], lanes, orders, rows
            )
            binned_ref[:, lanes] = jnp.concatenate(binned, 0)
        else:
            binned_ref[:, lanes] = jnp.zeros((orders * rows, chunk), jnp.float32)


def maps_kernel(
    efficiency_ref, legendre_ref, high_ref, low_ref, tables_ref, binned_ref, *refs,
    bins, orders, cycles_here, by_offset,
):
    *modes_refs, out_ref, left_ref, left_high_ref, sums_ref = refs
    degrees = legendre_ref.shape[2]
    shells = high_ref.shape[0]
    rows = 2 * bins
    bands = legendre_ref.shape[1] // cycles_here
    if by_offset:
        here = lax.axis_index("band")
        firsts = [((here ^ k) * cycles_here, cycles_here) for k in range(1, bands)]
        modes = jnp.concatenate([ref[...] for ref in modes_refs], 0)
    else:
        firsts = [(0, bands * cycles_here)]
        modes = modes_refs[0][...].reshape(bands * cycles_here, 2 * orders, shells)
    left, left_high = left_of(modes, efficiency_ref[...], orders, bins)
    left_ref[...] = left
    left_high_ref[...] = left_high

    def step(start, sums):
        lanes = pl.ds(start, TILE)
        binned = [binned_ref[pl.ds(m * rows, rows), lanes] for m in range(orders)]
        binned = add_cycles(
            binned, left_ref[...], left_high_ref[...], high_ref[:, lanes], low_ref[:, lanes],
            legendre_ref, firsts, lanes, orders, rows,
        )
        binned = jnp.concatenate(binned, 0)
        degree = (start + iota((rows, TILE), 1)).astype(jnp.float32)
        ratio = jnp.where(
            degree >= 2.0,
            jnp.sqrt((degree + 2.0) * (degree - 1.0) / jnp.maximum(degree * (degree + 1.0), 1.0)),
            0.0,
        )
        shear = (-jnp.concatenate([ratio] * orders, 0) * binned).astype(jnp.bfloat16)
        high, low = split(binned)
        return sums + lax.dot_general(
            jnp.concatenate([high, low, shear], 0),
            tables_ref[:, lanes],
            (((1,), (1,)), ((), ())),
            preferred_element_type=jnp.float32,
        )

    block = orders * cycles_here
    sums = jnp.zeros((3 * orders * rows, 4 * bands * block), jnp.float32)
    if by_offset:
        for start in range(0, degrees, TILE):
            sums = step(start, sums)
        sums_ref[...] = sums
    else:
        sums_ref[...] = sums

        @pl.loop(0, degrees // TILE)
        def _(i):
            sums_ref[...] = step(pl.multiple_of(i * TILE, TILE), sums_ref[...])

    width = 8 * block
    lane = iota((rows, width), 1)
    table = lane % (4 * block) // block
    order = lane % block // cycles_here
    first_half = iota((bins, width), 1) < 4 * block
    for pair in range(bands // 2):

        def own(kind):
            total = jnp.zeros((rows, width), jnp.float32)
            for m in range(orders):
                part = sums_ref[pl.ds((kind * orders + m) * rows, rows), pair * width : (pair + 1) * width]
                total = jnp.where(order == m, part, total)
            return total

        kappa = own(0) + jnp.where(table == KAPPA_HIGH, own(1), 0.0)
        value = jnp.where(table < PLUS, kappa, own(2))
        turned = pltpu.roll(value, 4 * block, 1)
        even = jnp.where(first_half, value[:bins], turned[bins:])
        odd = jnp.where(first_half, turned[:bins], value[bins:])
        for b in range(bins):
            out_ref[b * bands + 2 * pair] = even[b : b + 1]
            out_ref[b * bands + 2 * pair + 1] = odd[b : b + 1]


def unpack_kernel(got_ref, out_ref, *, bands, orders, cycles_here):
    width = got_ref.shape[2]
    groups = got_ref.shape[0] // bands
    block = orders * cycles_here
    own_order = iota((orders, width), 1) % block // cycles_here == iota((orders, width), 0)
    columns = []
    for z in range(bands):
        total = got_ref[z]
        for p in range(1, groups):
            total = total + got_ref[p * bands + z]
        columns.append(jnp.where(own_order, jnp.broadcast_to(total, (orders, width)), 0.0))
    values = jnp.concatenate(columns, 0)
    shape = (3 * cycles_here * 2, width)
    row, lane = iota(shape, 0), iota(shape, 1)
    field, cycle, part = row // (2 * cycles_here), row // 2 % cycles_here, row % 2
    lane_part, table = lane // (4 * block), lane // block % 4
    pick = jnp.where(
        field == 0,
        jnp.where((table <= KAPPA_LOW) & (lane_part == part), 1.0, 0.0),
        jnp.where(
            field == 1,
            jnp.where((table == PLUS) & (lane_part == part), 1.0, 0.0),
            jnp.where((table == MINUS) & (lane_part != part), jnp.where(part == 0, -1.0, 1.0), 0.0),
        ),
    )
    pick = jnp.where(lane % cycles_here == cycle, pick, 0.0)
    maps = lax.dot_general(
        pick, values, (((1,), (1,)), ((), ())),
        precision=lax.Precision.HIGHEST, preferred_element_type=jnp.float32,
    )
    for i in range(3 * cycles_here):
        out_ref[i] = maps[2 * i : 2 * i + 2]


def on_device(
    cycle_modes, cycle_weight, legendre, spin_plus, spin_minus, window, lensing, source_shell
):
    bands = lax.axis_size("band")
    shell_parts = lax.axis_size("shell")
    shells, cycles_here, _, orders_all = cycle_modes.shape
    orders, cycles, degrees = legendre.shape
    bins = source_shell.shape[0]
    assert bins == shell_parts and bands % 2 == 0
    by_offset = bands <= 4
    rows = 2 * bins
    columns = 4 * orders * cycles
    chunk = degrees // 4

    def shaped(*shape, dtype=jnp.float32):
        return jax.ShapeDtypeStruct(shape, dtype)

    block_shape = (cycles_here, 2 * orders, shells)
    pack = functools.partial(pack_kernel, bands=bands, orders=orders, by_offset=by_offset)
    operands = keep(cycle_modes.transpose(1, 2, 3, 0)), keep(cycle_weight.reshape(1, cycles_here))
    scratch = [
        pltpu.VMEM((bands, *block_shape), jnp.float32),
        pltpu.VMEM((cycles_here, 2, orders_all, shells), jnp.float32),
        pltpu.VMEM((1, cycles_here), jnp.float32),
        pltpu.SemaphoreType.DMA((2,)),
    ]
    if by_offset:
        own, *sends = pl.pallas_call(
            pack, in_specs=[HBM] * 2, out_specs=[VMEM] * bands, out_shape=[shaped(*block_shape)] * bands,
            scratch_shapes=scratch, compiler_params=PARAMS, name="pack",
        )(*operands)
        modes = [
            lax.ppermute(send, "band", [(z, z ^ k) for z in range(bands)])
            for k, send in enumerate(sends, 1)
        ]
        own = [own]
    else:
        blocks = pl.pallas_call(
            pack, in_specs=[HBM] * 2, out_specs=VMEM, out_shape=shaped(bands, *block_shape),
            scratch_shapes=scratch, compiler_params=PARAMS, name="pack",
        )(*operands)
        modes = [lax.all_to_all(blocks, "band", split_axis=0, concat_axis=0, tiled=True)]
        own = []
    prepared = pl.pallas_call(
        functools.partial(
            prepare_kernel, bins=bins, orders=orders, cycles=cycles, cycles_here=cycles_here,
            degrees=degrees, chunk=chunk, own=by_offset,
        ),
        in_specs=[HBM] * 6 + [VMEM] * len(own),
        out_specs=[VMEM] * 6,
        out_shape=[
            shaped(rows, shells), shaped(orders, cycles, degrees),
            shaped(shells, degrees, dtype=jnp.bfloat16), shaped(shells, degrees, dtype=jnp.bfloat16),
            shaped(columns, degrees, dtype=jnp.bfloat16), shaped(orders * rows, degrees),
        ],
        scratch_shapes=[
            pltpu.VMEM((shells, degrees), jnp.float32),
            pltpu.VMEM((orders, cycles, degrees), jnp.bfloat16),
            pltpu.VMEM((orders, cycles, degrees), jnp.bfloat16),
            pltpu.VMEM((1, bins), jnp.int32),
            pltpu.VMEM((1, shells), jnp.float32),
            pltpu.SemaphoreType.DMA((4, degrees // chunk)),
            pltpu.SemaphoreType.DMA((2,)),
        ],
        compiler_params=PARAMS,
        name="prepare",
    )(
        keep(source_shell.reshape(1, bins)), keep(lensing.reshape(1, shells)), keep(legendre),
        keep(spin_plus), keep(spin_minus), keep(window), *own,
    )
    arriving = orders * (cycles - cycles_here if by_offset else cycles) * rows
    maps = pl.pallas_call(
        functools.partial(maps_kernel, bins=bins, orders=orders, cycles_here=cycles_here, by_offset=by_offset),
        in_specs=[VMEM] * (6 + len(modes)),
        out_specs=VMEM,
        out_shape=shaped(bins * bands, 1, 8 * orders * cycles_here),
        scratch_shapes=[
            pltpu.VMEM((arriving, 2 * shells), jnp.bfloat16),
            pltpu.VMEM((arriving, shells), jnp.bfloat16),
            pltpu.VMEM((3 * orders * rows, columns), jnp.float32),
        ],
        compiler_params=PARAMS,
        name="maps",
    )(*prepared, *modes)
    got = lax.all_to_all(maps, ("shell", "band"), split_axis=0, concat_axis=0, tiled=True)
    out = pl.pallas_call(
        functools.partial(unpack_kernel, bands=bands, orders=orders, cycles_here=cycles_here),
        in_specs=[VMEM],
        out_specs=VMEM,
        out_shape=shaped(3 * cycles_here, 2, orders_all),
        compiler_params=PARAMS,
        name="unpack",
    )(got)
    return out.reshape(1, 3, cycles_here, 2, orders_all)


def solution(mesh):
    placed = (
        P(("cosmo", "shell"), "band", None, None),
        P("band"),
        P("band", None, None),
        P("band", None, None),
        P("band", None, None),
        P("shell", None),
        P(("cosmo", "shell")),
        P("cosmo"),
    )
    return jax.shard_map(
        on_device,
        mesh=mesh,
        in_specs=placed,
        out_specs=P(("cosmo", "shell"), None, "band", None, None),
        check_vma=False,
    )
```

time: 37.7 us -> 26.9 us (0.71)
  local copies, waits for them, and re-layouts: 9.54 us -> 0 us
  waiting for transfers between devices: 5.74 us -> 1.53 us
  Pallas kernels: 4.45 us -> 8.56 us
  other arithmetic: 1.69 us -> 0 us
  blocking collectives: 9.41 us -> 10.8 us
  starting transfers between devices: 6.35 us -> 5.71 us
    all_to_all x1 -> x0, starting transfers between devices: 6.35 us -> none  [on_device(): lax.all_to_all(weighted, 'band', split_axis=0, concat_axis=0, tiled=True)]
    unnamed x12 -> x0, local copies, waits for them, and re-layouts: 6.21 us -> none
    all_to_all x1 -> x0, waiting for transfers between devices: 5.74 us -> none  [on_device(): lax.all_to_all(weighted, 'band', split_axis=0, concat_axis=0, tiled=True)]
    ppermute x0 -> x3, starting transfers between devices: none -> 5.71 us  [on_device(): lax.ppermute(send, 'band', [(z, z ^ k) for z in range(bands)])]
    pallas_call x0 -> x3, Pallas kernels: none -> 5.69 us  [the longest x1 3.98 us: on_device(): pl.pallas_call(functools.partial(prepare_kernel, bins=bins, orders=orders...]
    reshape x4 -> x0, local copies, waits for them, and re-layouts: 1.95 us -> none  [the longest x2 0.96 us: on_device(): maps.reshape(3, 2, shell_parts, own_bins, orders, bands, cycles_here)]
    pallas_call x1, Pallas kernels: 4.45 us -> 2.87 us  [on_device(): pl.pallas_call(functools.partial(maps_kernel, bins=bins, orders=orders, c...]
    ppermute x0 -> x3, waiting for transfers between devices: none -> 1.53 us  [on_device(): lax.ppermute(send, 'band', [(z, z ^ k) for z in range(bands)])]
  transfers between devices with their start and end apart: 1 -> 3, of which waited for: 1 -> 1; matrix products, arithmetic and copies ran while one was open for 0% -> 0% of each run, Pallas kernels for 0% -> 15%
where the time goes in v2:
time: 26.9 us; the launch traced here: 26.7 us
  blocking collectives  10.8 us (40%)
  Pallas kernels  8.56 us (32%)
  starting transfers between devices  5.71 us (21%)
  waiting for transfers between devices  1.53 us (6%)
    all_to_all x1, blocking collectives, on_device(): lax.all_to_all(maps, ('shell', 'band'), split_axis=0, concat_axis=0, tile...  10.8 us
    ppermute x3, starting transfers between devices, on_device(): lax.ppermute(send, 'band', [(z, z ^ k) for z in range(bands)])  5.71 us
    pallas_call x1, Pallas kernels, on_device(): pl.pallas_call(functools.partial(prepare_kernel, bins=bins, orders=orders...  3.98 us
    pallas_call x1, Pallas kernels, on_device(): pl.pallas_call(functools.partial(maps_kernel, bins=bins, orders=orders, c...  2.87 us
    ppermute x3, waiting for transfers between devices, on_device(): lax.ppermute(send, 'band', [(z, z ^ k) for z in range(bands)])  1.53 us
    pallas_call x1, Pallas kernels, on_device(): pl.pallas_call(pack, in_specs=[HBM] * 2, out_specs=[VMEM] * bands, out_sh...  0.94 us
    pallas_call x1, Pallas kernels, on_device(): pl.pallas_call(functools.partial(unpack_kernel, bands=bands, orders=order...  0.77 us
  transfers between devices with their start and end apart: 3, of which 1 were waited for; matrix products, arithmetic and copies ran while one was open for 0% of the time, Pallas kernels for 15%

profile of v2, /device:TPU:0, one launch (start us, length us, event | category | flops | bytes accessed | tf_op | source)
XLA Modules:
  0.0 26.7 jit_solution(15421784271560183680)
XLA Ops:
  0.0 0.9 %pack.1 = (f32[4,8,128]{2,1,0:T(8,128)S(1)}, f32[4,8,128]{2,1,0:T(8,128)S(1)}, f32[4,8,128]{2,1,0:T(8,128)S(1)}, f32[4,8,128]{2,1,0:T(8,128)S(1)}) custom-call(f32[4,2,16,128]{3,2,1,0:T(8,128)} %bitcast.5, f32[1,4]{1,0:T(1,128)} %bitcast.6), custom_call_target="tpu_custom_call" | custom-call | tf_op jit(solution)/shard_map/pack/pallas_call | solution.py:310
  1.0 3.1 %collective-permute-start = (f32[4,8,128]{2,1,0:T(8,128)S(1)}, f32[4,8,128]{2,1,0:T(8,128)S(1)}, u32[]{:S(2)}, u32[]{:S(2)}) collective-permute-start(f32[4,8,128]{2,1,0:T(8,128)S(1)} %get-tuple-element.22), channel_id=1, source_target_pairs={{0,1},{1,0},{2,3},{3,2},{4,5},{5,4},{6,7},{7,6},{8,9},{9,8},{10,11... | collective-permute-start | bytes 49160 | tf_op jit(solution)/shard_map/ppermute | solution.py:315
  4.1 2.6 %collective-permute-start.1 = (f32[4,8,128]{2,1,0:T(8,128)S(1)}, f32[4,8,128]{2,1,0:T(8,128)S(1)}, u32[]{:S(2)}, u32[]{:S(2)}) collective-permute-start(f32[4,8,128]{2,1,0:T(8,128)S(1)} %get-tuple-element.23), channel_id=1, source_target_pairs={{0,2},{1,3},{2,0},{3,1},{4,6},{5,7},{6,4},{7,5},{8,10},{9,11},{10,... | collective-permute-start | bytes 49160 | tf_op jit(solution)/shard_map/ppermute | solution.py:315
  6.7 0.0 collective-permute-start.2
  6.7 4.0 %prepare.1 = (f32[8,128]{1,0:T(8,128)S(1)}, f32[4,16,4096]{2,1,0:T(8,128)S(1)}, bf16[128,4096]{1,0:T(8,128)(2,1)S(1)}, bf16[128,4096]{1,0:T(8,128)(2,1)S(1)}, bf...) custom-call(s32[1,4]{1,0:T(1,128)} %bitcast.7, f32[1,128]{1,0:T(1,128)} %bitcast.8, f32[4,16,4096]{2,1,0:T(8,128)} %legendre_in.1, ...), custom_call_target="tpu_custom_call" | custom-call | tf_op jit(solution)/shard_map/prepare/pallas_call | solution.py:326
  10.7 0.0 collective-permute-done.refs_0_
  10.7 0.0 collective-permute-done.1.refs_1_
  10.7 1.5 %collective-permute-done.2.refs_2_ = f32[4,8,128]{2,1,0:T(8,128)S(1)} collective-permute-done((f32[4,8,128]{2,1,0:T(8,128)S(1)}, f32[4,8,128]{2,1,0:T(8,128)S(1)}, u32[]{:S(2)}, u32[]{:S(2)}) %collective-permute-start.2) | collective-permute-done | bytes 16416 | tf_op jit(solution)/shard_map/ppermute | solution.py:315
  12.2 2.9 %maps.1 = f32[16,1,128]{2,1,0:T(1,128)S(1)} custom-call(f32[8,128]{1,0:T(8,128)S(1)} %get-tuple-element.16.efficiency_ref, f32[4,16,4096]{2,1,0:T(8,128)S(1)} %get-tuple-element.17.legendre_ref, bf16[128,4096]{1,0:T(8,128)(2,1)S(1)} %get-tuple-element.18.high_ref, bf16[128,4096]{1,0:T(8,128)(2,1)S(1)} %get-tuple-element.19.low_ref, ...), custom_call_target="tpu_custom_call" | custom-call | tf_op jit(solution)/shard_map/maps/pallas_call | solution.py:354
  15.1 10.8 %all_to_all.5.got_ref = f32[16,1,128]{2,1,0:T(1,128)S(1)} all-to-all(f32[16,1,128]{2,1,0:T(1,128)S(1)} %maps.1), channel_id=1, replica_groups=mesh['cosmo'=2,'shell'=4,'band'=4] {'shell','band'}, dimensions={0} | all-to-all | bytes 16384 | tf_op jit(solution)/shard_map/all_to_all | solution.py:367
  25.9 0.8 %unpack.1 = f32[12,2,16]{2,1,0:T(2,128)} custom-call(f32[16,1,128]{2,1,0:T(1,128)S(1)} %all_to_all.5.got_ref), custom_call_target="tpu_custom_call" | custom-call | tf_op jit(solution)/shard_map/unpack/pallas_call | solution.py:368
Async XLA Ops:
  1.0 9.7 %collective-permute-start = (f32[4,8,128]{2,1,0:T(8,128)S(1)}, f32[4,8,128]{2,1,0:T(8,128)S(1)}, u32[]{:S(2)}, u32[]{:S(2)}) collective-permute-start(f32[4,8,128]{2,1,0:T(8,128)S(1)} %get-tuple-element.22), channel_id=1, source_target_pairs={{0,1},{1,0},{2,3},{3,2},{4,5},{5,4},{6,7},{7,6},{8,9},{9,8},{10,11... | collective-permute-start | bytes 49160 | tf_op jit(solution)/shard_map/ppermute | solution.py:315
  4.1 6.6 %collective-permute-start.1 = (f32[4,8,128]{2,1,0:T(8,128)S(1)}, f32[4,8,128]{2,1,0:T(8,128)S(1)}, u32[]{:S(2)}, u32[]{:S(2)}) collective-permute-start(f32[4,8,128]{2,1,0:T(8,128)S(1)} %get-tuple-element.23), channel_id=1, source_target_pairs={{0,2},{1,3},{2,0},{3,1},{4,6},{5,7},{6,4},{7,5},{8,10},{9,11},{10,... | collective-permute-start | bytes 49160 | tf_op jit(solution)/shard_map/ppermute | solution.py:315
  6.7 5.5 %collective-permute-start.2 = (f32[4,8,128]{2,1,0:T(8,128)S(1)}, f32[4,8,128]{2,1,0:T(8,128)S(1)}, u32[]{:S(2)}, u32[]{:S(2)}) collective-permute-start(f32[4,8,128]{2,1,0:T(8,128)S(1)} %get-tuple-element.24), channel_id=1, source_target_pairs={{0,3},{1,2},{2,1},{3,0},{4,7},{5,6},{6,5},{7,4},{8,11},{9,10},{10,... | collective-permute-start | bytes 49160 | tf_op jit(solution)/shard_map/ppermute | solution.py:315

commit v3 on v0

v3 whole, which is shorter than its diff:
```python
import functools

import jax
import jax.numpy as jnp
from jax import lax
from jax.experimental import pallas as pl
from jax.experimental.pallas import tpu as pltpu
from jax.sharding import PartitionSpec as P

TILE = 512
VMEM = pl.BlockSpec(memory_space=pltpu.VMEM)
HBM = pl.BlockSpec(memory_space=pltpu.HBM)
PARAMS = pltpu.CompilerParams(vmem_limit_bytes=28 * 2**20)
KAPPA_HIGH, KAPPA_LOW, PLUS, MINUS = range(4)


def keep(x):
    return pltpu.with_memory_space_constraint(x, pltpu.HBM)


def split(x):
    high = x.astype(jnp.bfloat16)
    low = (x - high.astype(jnp.float32)).astype(jnp.bfloat16)
    return high, low


def iota(shape, axis):
    return lax.broadcasted_iota(jnp.int32, shape, axis)


def pack_kernel(
    modes_in, weight_in, source_in, lensing_in, *refs, bands, orders, bins, offsets,
):
    *out_refs, efficiency_ref, blocks_ref, modes_ref, weight_ref, source_ref, lensing_ref, sems = refs
    cycles_here, _, _, shells = modes_ref.shape
    pairs = (
        (modes_in, modes_ref), (weight_in, weight_ref), (source_in, source_ref), (lensing_in, lensing_ref),
    )
    copies = [pltpu.make_async_copy(*pair, sems.at[i]) for i, pair in enumerate(pairs)]
    for copy in copies:
        copy.start()
    for copy in copies:
        copy.wait()
    for r in range(cycles_here):
        weight = jnp.broadcast_to(weight_ref[0:1, r : r + 1], (orders, shells))
        for c in range(2):
            for z in range(bands):
                blocks_ref[z, r, c * orders : (c + 1) * orders, :] = (
                    modes_ref[r, c, z * orders : (z + 1) * orders, :] * weight
                )
    if offsets:
        here = lax.axis_index("band")
        for k, out_ref in zip((0, *offsets), out_refs):
            out_ref[...] = blocks_ref[here ^ k]
    else:
        out_refs[0][...] = blocks_ref[...]
    rows = 2 * bins
    row_bin = iota((rows, shells), 0) % bins
    source = jnp.zeros((rows, shells), jnp.int32)
    for b in range(bins):
        source = jnp.where(row_bin == b, jnp.broadcast_to(source_ref[0:1, b : b + 1], (rows, shells)), source)
    shell_ids = lax.axis_index("shell") * shells + iota((rows, shells), 1)
    efficiency_ref[...] = (
        lensing_ref[...]
        * jnp.maximum(source - shell_ids, 0).astype(jnp.float32)
        / (source + 1).astype(jnp.float32)
    )


def left_of(modes, efficiency, orders, bins):
    cycles, _, shells = modes.shape
    rows = 2 * bins
    first_part = (iota((1, rows, shells), 1) < bins)
    parts = []
    for m in range(orders):
        real = jnp.broadcast_to(modes[:, m : m + 1, :], (cycles, rows, shells))
        imag = jnp.broadcast_to(modes[:, orders + m : orders + m + 1, :], (cycles, rows, shells))
        left = jnp.where(first_part, real, imag) * efficiency[None]
        parts.append(left.reshape(cycles * rows, shells))
    high, low = split(jnp.concatenate(parts, 0))
    return jnp.concatenate([high, low], 1), high


def add_cycles(binned, left, left_high, high, low, legendre_ref, firsts, lanes, orders, rows):
    product = jnp.dot(left, jnp.concatenate([high, high], 0), preferred_element_type=jnp.float32)
    product = product + jnp.dot(left_high, low, preferred_element_type=jnp.float32)
    out = []
    at = 0
    for m in range(orders):
        total = binned[m]
        for first, count in firsts:
            for r in range(count):
                total = total + legendre_ref[m, pl.ds(first + r, 1), lanes] * product[at : at + rows]
                at += rows
        out.append(total)
    return out


def prepare_kernel(window_ref, legendre_ref, high_ref, low_ref, table_high_ref, table_low_ref):
    high_ref[...], low_ref[...] = split(window_ref[...])
    table_high_ref[...], table_low_ref[...] = split(legendre_ref[...])


def each_tile(degrees, unroll, step):
    if unroll:
        for start in range(0, degrees, TILE):
            step(start)
    else:
        pl.loop(0, degrees // TILE)(lambda i: step(pl.multiple_of(i * TILE, TILE)))


def gather_left(modes_refs, efficiency_ref, left_ref, left_high_ref, orders, cycles_here, offsets):
    if offsets:
        here = lax.axis_index("band")
        firsts = [((here ^ k) * cycles_here, cycles_here) for k in offsets]
        modes = jnp.concatenate([ref[...] for ref in modes_refs], 0)
    else:
        modes = modes_refs[0][...]
        modes = modes.reshape(-1, *modes.shape[2:])
        firsts = [(0, modes.shape[0])]
    left_ref[...], left_high_ref[...] = left_of(
        modes, efficiency_ref[...], orders, efficiency_ref.shape[0] // 2
    )
    return firsts


def first_kernel(
    efficiency_ref, legendre_ref, high_ref, low_ref, *refs, orders, cycles_here, offsets,
):
    *modes_refs, binned_ref, left_ref, left_high_ref = refs
    rows = efficiency_ref.shape[0]
    firsts = gather_left(modes_refs, efficiency_ref, left_ref, left_high_ref, orders, cycles_here, offsets)

    def step(start):
        lanes = pl.ds(start, TILE)
        binned = add_cycles(
            [jnp.zeros((rows, TILE), jnp.float32)] * orders, left_ref[...], left_high_ref[...],
            high_ref[:, lanes], low_ref[:, lanes], legendre_ref, firsts, lanes, orders, rows,
        )
        for m in range(orders):
            binned_ref[pl.ds(m * rows, rows), lanes] = binned[m]

    each_tile(legendre_ref.shape[2], True, step)


def maps_kernel(
    efficiency_ref, legendre_ref, high_ref, low_ref, table_high_ref, table_low_ref, plus_ref, minus_ref, *refs,
    bands, orders, cycles_here, offsets,
):
    if offsets:
        binned_ref, *refs = refs
    *modes_refs, out_ref, left_ref, left_high_ref, sums_ref = refs
    cycles = legendre_ref.shape[1]
    rows = efficiency_ref.shape[0]
    bins = rows // 2
    columns = orders * cycles
    firsts = gather_left(modes_refs, efficiency_ref, left_ref, left_high_ref, orders, cycles_here, offsets)
    sums_ref[...] = jnp.zeros(sums_ref.shape, jnp.float32)

    def step(start):
        lanes = pl.ds(start, TILE)
        if offsets:
            binned = [binned_ref[pl.ds(m * rows, rows), lanes] for m in range(orders)]
        else:
            binned = [jnp.zeros((rows, TILE), jnp.float32)] * orders
        binned = add_cycles(
            binned, left_ref[...], left_high_ref[...], high_ref[:, lanes], low_ref[:, lanes],
            legendre_ref, firsts, lanes, orders, rows,
        )
        binned = jnp.concatenate(binned, 0)
        degree = (start + iota((rows, TILE), 1)).astype(jnp.float32)
        ratio = jnp.where(
            degree >= 2.0,
            jnp.sqrt((degree + 2.0) * (degree - 1.0) / jnp.maximum(degree * (degree + 1.0), 1.0)),
            0.0,
        )
        shear = (-jnp.concatenate([ratio] * orders, 0) * binned).astype(jnp.bfloat16)
        high, low = split(binned)
        tables = [
            ref[:, :, lanes].reshape(columns, TILE)
            for ref in (table_high_ref, table_low_ref, plus_ref, minus_ref)
        ]
        sums_ref[...] += lax.dot_general(
            jnp.concatenate([high, low, shear], 0), jnp.concatenate(tables, 0),
            (((1,), (1,)), ((), ())),
            preferred_element_type=jnp.float32,
        )

    each_tile(legendre_ref.shape[2], bool(offsets), step)

    lane = iota((rows, 4 * columns), 1)
    table = lane // columns
    order = lane % columns // cycles

    def own(kind):
        total = jnp.zeros((rows, 4 * columns), jnp.float32)
        for m in range(orders):
            total = jnp.where(order == m, sums_ref[pl.ds((kind * orders + m) * rows, rows), :], total)
        return total

    kappa = own(0) + jnp.where(table == KAPPA_HIGH, own(1), 0.0)
    value = jnp.where(table < PLUS, kappa, own(2))
    for b in range(bins):
        for z in range(bands):
            for c in range(2):
                out_ref[b * bands + z, c : c + 1, :] = value[c * bins + b : c * bins + b + 1]


def unpack_kernel(got_ref, out_ref, *, bands, orders, cycles_here):
    width = got_ref.shape[2]
    groups = got_ref.shape[0] // bands
    cycles = bands * cycles_here
    columns = orders * cycles
    own_order = iota((orders, width), 1) % columns // cycles == iota((orders, width), 0)
    shape = (3 * cycles_here * 2, width)
    row, lane = iota(shape, 0), iota(shape, 1)
    field, cycle, part = row // (2 * cycles_here), row // 2 % cycles_here, row % 2
    table = lane // columns
    here = lane % cycles == lax.axis_index("band") * cycles_here + cycle
    total = [got_ref[z] for z in range(bands)]
    for p in range(1, groups):
        total = [total[z] + got_ref[p * bands + z] for z in range(bands)]
    maps = jnp.zeros((3 * cycles_here * 2, bands * orders), jnp.float32)
    for c in range(2):
        values = jnp.concatenate(
            [
                jnp.where(own_order, jnp.broadcast_to(total[z][c : c + 1], (orders, width)), 0.0)
                for z in range(bands)
            ],
            0,
        )
        same = jnp.where(part == c, 1.0, 0.0)
        other = jnp.where(part == c, 0.0, 1.0 if c == 0 else -1.0)
        pick = jnp.where(
            field == 0,
            jnp.where(table <= KAPPA_LOW, same, 0.0),
            jnp.where(field == 1, jnp.where(table == PLUS, same, 0.0), jnp.where(table == MINUS, other, 0.0)),
        )
        maps = maps + lax.dot_general(
            jnp.where(here, pick, 0.0), values, (((1,), (1,)), ((), ())),
            precision=lax.Precision.HIGHEST, preferred_element_type=jnp.float32,
        )
    for i in range(3 * cycles_here):
        out_ref[i] = maps[2 * i : 2 * i + 2]


def on_device(
    cycle_modes, cycle_weight, legendre, spin_plus, spin_minus, window, lensing, source_shell
):
    bands = lax.axis_size("band")
    shell_parts = lax.axis_size("shell")
    shells, cycles_here, _, orders_all = cycle_modes.shape
    orders, cycles, degrees = legendre.shape
    bins = source_shell.shape[0]
    assert bins == shell_parts
    offsets = (2, 3, 1) if bands == 4 else ()
    rows = 2 * bins
    columns = 4 * orders * cycles

    def shaped(*shape, dtype=jnp.float32):
        return jax.ShapeDtypeStruct(shape, dtype)

    def left_scratch(blocks):
        return [
            pltpu.VMEM((orders * blocks * cycles_here * rows, 2 * shells), jnp.bfloat16),
            pltpu.VMEM((orders * blocks * cycles_here * rows, shells), jnp.bfloat16),
        ]

    block_shape = (cycles_here, 2 * orders, shells)
    out_shape = [shaped(*block_shape)] * bands if offsets else [shaped(bands, *block_shape)]
    out_shape = [*out_shape, shaped(rows, shells)]
    *blocks, efficiency = pl.pallas_call(
        functools.partial(pack_kernel, bands=bands, orders=orders, bins=bins, offsets=offsets),
        in_specs=[HBM] * 4,
        out_specs=[VMEM] * len(out_shape),
        out_shape=out_shape,
        scratch_shapes=[
            pltpu.VMEM((bands, *block_shape), jnp.float32),
            pltpu.VMEM((cycles_here, 2, orders_all, shells), jnp.float32),
            pltpu.VMEM((1, cycles_here), jnp.float32),
            pltpu.VMEM((1, bins), jnp.int32),
            pltpu.VMEM((1, shells), jnp.float32),
            pltpu.SemaphoreType.DMA((4,)),
        ],
        compiler_params=PARAMS,
        cost_estimate=pl.CostEstimate(flops=10**10, bytes_accessed=2**17, transcendentals=0),
        name="pack",
    )(
        keep(cycle_modes.transpose(1, 2, 3, 0)), keep(cycle_weight.reshape(1, cycles_here)),
        keep(source_shell.reshape(1, bins)), keep(lensing.reshape(1, shells)),
    )
    if offsets:
        own, *sends = blocks
        got = [
            lax.ppermute(send, "band", [(z, z ^ k) for z in range(bands)])
            for k, send in zip(offsets, sends)
        ]
    else:
        got = [lax.all_to_all(blocks[0], "band", split_axis=0, concat_axis=0, tiled=True)]
    half = jnp.bfloat16
    high, low, table_high, table_low = pl.pallas_call(
        prepare_kernel,
        in_specs=[VMEM] * 2,
        out_specs=[VMEM] * 4,
        out_shape=[shaped(shells, degrees, dtype=half)] * 2 + [shaped(orders, cycles, degrees, dtype=half)] * 2,
        compiler_params=PARAMS,
        name="prepare",
    )(window, legendre)
    operands = [efficiency, legendre, high, low, table_high, table_low, spin_plus, spin_minus]
    last = got
    if offsets:
        last = got[1:]
        operands.append(
            pl.pallas_call(
                functools.partial(
                    first_kernel, orders=orders, cycles_here=cycles_here, offsets=(0, offsets[0])
                ),
                in_specs=[VMEM] * 6,
                out_specs=VMEM,
                out_shape=shaped(orders * rows, degrees),
                scratch_shapes=left_scratch(2),
                compiler_params=PARAMS,
                name="first",
            )(efficiency, legendre, high, low, own, got[0])
        )
    operands += last
    maps = pl.pallas_call(
        functools.partial(
            maps_kernel, bands=bands, orders=orders, cycles_here=cycles_here, offsets=offsets[1:]
        ),
        in_specs=[VMEM] * len(operands),
        out_specs=VMEM,
        out_shape=shaped(bins * bands, 2, columns),
        scratch_shapes=[
            *left_scratch(len(last) if offsets else bands),
            pltpu.VMEM((3 * orders * rows, columns), jnp.float32),
        ],
        compiler_params=PARAMS,
        name="maps",
    )(*operands)
    got = lax.all_to_all(maps, ("shell", "band"), split_axis=0, concat_axis=0, tiled=True)
    out = pl.pallas_call(
        functools.partial(unpack_kernel, bands=bands, orders=orders, cycles_here=cycles_here),
        in_specs=[VMEM],
        out_specs=VMEM,
        out_shape=shaped(3 * cycles_here, 2, orders_all),
        compiler_params=PARAMS,
        name="unpack",
    )(got)
    return out.reshape(1, 3, cycles_here, 2, orders_all)


def solution(mesh):
    placed = (
        P(("cosmo", "shell"), "band", None, None),
        P("band"),
        P("band", None, None),
        P("band", None, None),
        P("band", None, None),
        P("shell", None),
        P(("cosmo", "shell")),
        P("cosmo"),
    )
    return jax.shard_map(
        on_device,
        mesh=mesh,
        in_specs=placed,
        out_specs=P(("cosmo", "shell"), None, "band", None, None),
        check_vma=False,
    )
```

time: 59.1 us -> 24.8 us (0.42)
  matrix products: 24.6 us -> 0 us
  blocking collectives: 18.6 us -> 10.6 us
  Pallas kernels: 0 us -> 5.99 us
  local copies, waits for them, and re-layouts: 3.45 us -> 0.02 us
  other arithmetic: 1.78 us -> 0 us
  waiting for transfers between devices: 3.8 us -> 2.17 us
  starting transfers between devices: 6.35 us -> 5.71 us
    dot_general x5 -> x0, matrix products: 24.6 us -> none  [the longest x1 13.5 us: on_device(): jnp.einsum('nrcm,mrl->nmcl', lax.all_to_all(weighted, 'band', split_axis=...]
    unnamed x1 -> x0, blocking collectives: 10.5 us -> none
    all_to_all x1 -> x0, starting transfers between devices: 6.35 us -> none  [on_device(): lax.all_to_all(weighted, 'band', split_axis=3, concat_axis=1, tiled=True)]
    pallas_call x0 -> x5, Pallas kernels: none -> 5.99 us  [the longest x1 2.32 us: on_device(): pl.pallas_call(functools.partial(maps_kernel, bands=bands, orders=orders,...]
    ppermute x0 -> x3, starting transfers between devices: none -> 5.71 us  [on_device(): lax.ppermute(send, 'band', [(z, z ^ k) for z in range(bands)])]
    all_to_all x1 -> x0, waiting for transfers between devices: 3.8 us -> none  [on_device(): lax.all_to_all(weighted, 'band', split_axis=3, concat_axis=1, tiled=True)]
    all_to_all x1, blocking collectives: 8.06 us -> 10.6 us  [on_device(): lax.all_to_all(maps, ('shell', 'band'), split_axis=0, concat_axis=0, tile...]
    ppermute x0 -> x3, waiting for transfers between devices: none -> 2.17 us  [on_device(): lax.ppermute(send, 'band', [(z, z ^ k) for z in range(bands)])]
  transfers between devices with their start and end apart: 1 -> 3, of which waited for: 1 -> 1; matrix products, arithmetic and copies ran while one was open for 3% -> 0% of each run, Pallas kernels for 0% -> 7%
where the time goes in v3:
time: 24.8 us; the launch traced here: 24.6 us
  blocking collectives  10.6 us (43%)
  Pallas kernels  5.99 us (24%)
  starting transfers between devices  5.71 us (23%)
  waiting for transfers between devices  2.17 us (9%)
    all_to_all x1, blocking collectives, on_device(): lax.all_to_all(maps, ('shell', 'band'), split_axis=0, concat_axis=0, tile...  10.6 us
    ppermute x3, starting transfers between devices, on_device(): lax.ppermute(send, 'band', [(z, z ^ k) for z in range(bands)])  5.71 us
    pallas_call x1, Pallas kernels, on_device(): pl.pallas_call(functools.partial(maps_kernel, bands=bands, orders=orders,...  2.32 us
    ppermute x3, waiting for transfers between devices, on_device(): lax.ppermute(send, 'band', [(z, z ^ k) for z in range(bands)])  2.17 us
    pallas_call x1, Pallas kernels, on_device(): pl.pallas_call(functools.partial(first_kernel, orders=orders, cycles_here...  1.25 us
    pallas_call x1, Pallas kernels, on_device(): pl.pallas_call(functools.partial(pack_kernel, bands=bands, orders=orders,...  1.12 us
    pallas_call x1, Pallas kernels, on_device(): pl.pallas_call(functools.partial(unpack_kernel, bands=bands, orders=order...  0.81 us
  transfers between devices with their start and end apart: 3, of which 1 were waited for; matrix products, arithmetic and copies ran while one was open for 0% of the time, Pallas kernels for 7%

profile of v3, /device:TPU:0, one launch (start us, length us, event | category | flops | bytes accessed | tf_op | source)
XLA Modules:
  0.0 24.6 jit_solution(12568041195659785181)
XLA Ops:
  0.0 0.0 copy-start
  0.0 0.0 copy-start.1
  0.0 1.1 %pack.1 = (f32[4,8,128]{2,1,0:T(8,128)S(1)}, f32[4,8,128]{2,1,0:T(8,128)S(1)}, f32[4,8,128]{2,1,0:T(8,128)S(1)}, f32[4,8,128]{2,1,0:T(8,128)S(1)}, f32[8,128]{1,0:T(8,128)S(1)}) custom-call(f32[4,2,16,128]{3,2,1,0:T(8,128)} %bitcast.5, f32[1,4]{1,0:T(1,128)} %bitcast.6, s32[1,4]{1,0:T(1,128)} %bitcast.7, f32[1,128]{1,0:T(1,128)} %bitcast.8), custom_call_target="tpu_custom_call" | custom-call | flops 10000000000 | bytes 131072 | tf_op jit(solution)/shard_map/pack/pallas_call | solution.py:272
  1.1 4.1 %collective-permute-start = (f32[4,8,128]{2,1,0:T(8,128)S(1)}, f32[4,8,128]{2,1,0:T(8,128)S(1)}, u32[]{:S(2)}, u32[]{:S(2)}) collective-permute-start(f32[4,8,128]{2,1,0:T(8,128)S(1)} %get-tuple-element.20), channel_id=1, source_target_pairs={{0,2},{1,3},{2,0},{3,1},{4,6},{5,7},{6,4},{7,5},{8,10},{9,11},{10,... | collective-permute-start | bytes 49160 | tf_op jit(solution)/shard_map/ppermute | solution.py:295
  5.3 1.3 %collective-permute-start.1 = (f32[4,8,128]{2,1,0:T(8,128)S(1)}, f32[4,8,128]{2,1,0:T(8,128)S(1)}, u32[]{:S(2)}, u32[]{:S(2)}) collective-permute-start(f32[4,8,128]{2,1,0:T(8,128)S(1)} %get-tuple-element.21), channel_id=1, source_target_pairs={{0,3},{1,2},{2,1},{3,0},{4,7},{5,6},{6,5},{7,4},{8,11},{9,10},{10,... | collective-permute-start | bytes 49160 | tf_op jit(solution)/shard_map/ppermute | solution.py:295
  6.6 0.2 collective-permute-start.2
  6.8 0.0 copy-done
  6.8 0.0 copy-done.1
  6.8 0.5 %prepare.1 = (bf16[128,4096]{1,0:T(8,128)(2,1)S(1)}, bf16[128,4096]{1,0:T(8,128)(2,1)S(1)}, bf16[4,16,4096]{2,1,0:T(8,128)(2,1)S(1)}, bf16[4,16,4096]{2,1,0:T(8,128)(2,1)S(1)}) custom-call(f32[128,4096]{1,0:T(8,128)S(1)} %copy-done.1, f32[4,16,4096]{2,1,0:T(8,128)S(1)} %copy-done), custom_call_target="tpu_custom_call" | custom-call | tf_op jit(solution)/shard_map/prepare/pallas_call | solution.py:301
  7.3 0.0 copy-start.2
  7.4 0.0 copy-start.3
  7.4 0.0 collective-permute-done.refs_1_
  7.4 1.2 %first.1.refs_0_ = f32[32,4096]{1,0:T(8,128)S(1)} custom-call(f32[8,128]{1,0:T(8,128)S(1)} %get-tuple-element.14.efficiency_ref, f32[4,16,4096]{2,1,0:T(8,128)S(1)} %copy-done, bf16[128,4096]{1,0:T(8,128)(2,1)S(1)} %get-tuple-element.15.high_ref, bf16[128,4096]{1,0:T(8,128)(2,1)S(1)} %get-tuple-element.16.low_ref, ...), custom_call_target="tpu_custom_call" | custom-call | tf_op jit(solution)/shard_map/first/pallas_call | solution.py:314
  8.6 2.2 %collective-permute-done.1.refs_1_ = f32[4,8,128]{2,1,0:T(8,128)S(1)} collective-permute-done((f32[4,8,128]{2,1,0:T(8,128)S(1)}, f32[4,8,128]{2,1,0:T(8,128)S(1)}, u32[]{:S(2)}, u32[]{:S(2)}) %collective-permute-start.1) | collective-permute-done | bytes 16416 | tf_op jit(solution)/shard_map/ppermute | solution.py:295
  10.8 0.0 collective-permute-done.2.refs_2_
  10.8 0.0 copy-done.2
  10.8 0.0 copy-done.3
  10.8 2.3 %maps.1 = f32[16,2,256]{2,1,0:T(2,128)S(1)} custom-call(f32[8,128]{1,0:T(8,128)S(1)} %get-tuple-element.14.efficiency_ref, f32[4,16,4096]{2,1,0:T(8,128)S(1)} %copy-done, bf16[128,4096]{1,0:T(8,128)(2,1)S(1)} %get-tuple-element.15.high_ref, bf16[128,4096]{1,0:T(8,128)(2,1)S(1)} %get-tuple-element.16.low_ref, ...), custom_call_target="tpu_custom_call" | custom-call | tf_op jit(solution)/shard_map/maps/pallas_call | solution.py:327
  13.1 10.6 %all_to_all.5.got_ref = f32[16,2,256]{2,1,0:T(2,128)S(1)} all-to-all(f32[16,2,256]{2,1,0:T(2,128)S(1)} %maps.1), channel_id=1, replica_groups=mesh['cosmo'=2,'shell'=4,'band'=4] {'shell','band'}, dimensions={0} | all-to-all | bytes 65536 | tf_op jit(solution)/shard_map/all_to_all | solution.py:341
  23.8 0.8 %unpack.1 = f32[12,2,16]{2,1,0:T(2,128)} custom-call(f32[16,2,256]{2,1,0:T(2,128)S(1)} %all_to_all.5.got_ref), custom_call_target="tpu_custom_call" | custom-call | tf_op jit(solution)/shard_map/unpack/pallas_call | solution.py:342
Async XLA Ops:
  0.0 6.8 %copy-start = (f32[4,16,4096]{2,1,0:T(8,128)S(1)}, f32[4,16,4096]{2,1,0:T(8,128)}, u32[]{:S(2)}) copy-start(f32[4,16,4096]{2,1,0:T(8,128)} %legendre_ref.5) | copy-start | bytes 3145732
  0.0 6.8 %copy-start.1 = (f32[128,4096]{1,0:T(8,128)S(1)}, f32[128,4096]{1,0:T(8,128)}, u32[]{:S(2)}) copy-start(f32[128,4096]{1,0:T(8,128)} %window_ref.1) | copy-start | bytes 6291460
  1.1 6.2 %collective-permute-start = (f32[4,8,128]{2,1,0:T(8,128)S(1)}, f32[4,8,128]{2,1,0:T(8,128)S(1)}, u32[]{:S(2)}, u32[]{:S(2)}) collective-permute-start(f32[4,8,128]{2,1,0:T(8,128)S(1)} %get-tuple-element.20), channel_id=1, source_target_pairs={{0,2},{1,3},{2,0},{3,1},{4,6},{5,7},{6,4},{7,5},{8,10},{9,11},{10,... | collective-permute-start | bytes 49160 | tf_op jit(solution)/shard_map/ppermute | solution.py:295
  5.3 5.5 %collective-permute-start.1 = (f32[4,8,128]{2,1,0:T(8,128)S(1)}, f32[4,8,128]{2,1,0:T(8,128)S(1)}, u32[]{:S(2)}, u32[]{:S(2)}) collective-permute-start(f32[4,8,128]{2,1,0:T(8,128)S(1)} %get-tuple-element.21), channel_id=1, source_target_pairs={{0,3},{1,2},{2,1},{3,0},{4,7},{5,6},{6,5},{7,4},{8,11},{9,10},{10,... | collective-permute-start | bytes 49160 | tf_op jit(solution)/shard_map/ppermute | solution.py:295
  6.6 4.2 %collective-permute-start.2 = (f32[4,8,128]{2,1,0:T(8,128)S(1)}, f32[4,8,128]{2,1,0:T(8,128)S(1)}, u32[]{:S(2)}, u32[]{:S(2)}) collective-permute-start(f32[4,8,128]{2,1,0:T(8,128)S(1)} %get-tuple-element.22), channel_id=1, source_target_pairs={{0,1},{1,0},{2,3},{3,2},{4,5},{5,4},{6,7},{7,6},{8,9},{9,8},{10,11... | collective-permute-start | bytes 49160 | tf_op jit(solution)/shard_map/ppermute | solution.py:295
  7.3 3.5 %copy-start.2 = (bf16[4,16,4096]{2,1,0:T(8,128)(2,1)S(1)}, bf16[4,16,4096]{2,1,0:T(8,128)(2,1)}, u32[]{:S(2)}) copy-start(bf16[4,16,4096]{2,1,0:T(8,128)(2,1)} %plus_ref.1) | copy-start | bytes 1572868
  7.4 3.5 %copy-start.3 = (bf16[4,16,4096]{2,1,0:T(8,128)(2,1)S(1)}, bf16[4,16,4096]{2,1,0:T(8,128)(2,1)}, u32[]{:S(2)}) copy-start(bf16[4,16,4096]{2,1,0:T(8,128)(2,1)} %minus_ref.1) | copy-start | bytes 1572868

commit v4 on v3

--- a/solution.py
+++ b/solution.py
@@ -7,7 +7,8 @@
 from jax.experimental.pallas import tpu as pltpu
 from jax.sharding import PartitionSpec as P
 
-TILE = 512
+TILE = 256
+LANES = 128
 VMEM = pl.BlockSpec(memory_space=pltpu.VMEM)
 HBM = pl.BlockSpec(memory_space=pltpu.HBM)
 PARAMS = pltpu.CompilerParams(vmem_limit_bytes=28 * 2**20)
@@ -28,19 +29,18 @@
     return lax.broadcasted_iota(jnp.int32, shape, axis)
 
 
-def pack_kernel(
-    modes_in, weight_in, source_in, lensing_in, *refs, bands, orders, bins, offsets,
-):
-    *out_refs, efficiency_ref, blocks_ref, modes_ref, weight_ref, source_ref, lensing_ref, sems = refs
-    cycles_here, _, _, shells = modes_ref.shape
-    pairs = (
-        (modes_in, modes_ref), (weight_in, weight_ref), (source_in, source_ref), (lensing_in, lensing_ref),
-    )
-    copies = [pltpu.make_async_copy(*pair, sems.at[i]) for i, pair in enumerate(pairs)]
+def load_kernel(*refs):
+    count = len(refs) // 2
+    copies = [pltpu.make_async_copy(refs[i], refs[count + i], refs[-1].at[i]) for i in range(count)]
     for copy in copies:
         copy.start()
     for copy in copies:
         copy.wait()
+
+
+def pack_kernel(modes_ref, weight_ref, source_ref, lensing_ref, *refs, bands, orders, bins, offsets):
+    *out_refs, efficiency_ref, blocks_ref = refs
+    cycles_here, _, _, shells = modes_ref.shape
     for r in range(cycles_here):
         weight = jnp.broadcast_to(weight_ref[0:1, r : r + 1], (orders, shells))
         for c in range(2):
@@ -96,11 +96,6 @@
     return out
 
 
-def prepare_kernel(window_ref, legendre_ref, high_ref, low_ref, table_high_ref, table_low_ref):
-    high_ref[...], low_ref[...] = split(window_ref[...])
-    table_high_ref[...], table_low_ref[...] = split(legendre_ref[...])
-
-
 def each_tile(degrees, unroll, step):
     if unroll:
         for start in range(0, degrees, TILE):
@@ -124,17 +119,43 @@
     return firsts
 
 
-def first_kernel(
-    efficiency_ref, legendre_ref, high_ref, low_ref, *refs, orders, cycles_here, offsets,
+def prepare_kernel(window_ref, legendre_ref, plus_ref, minus_ref, *refs, orders, cycles_here):
+    if len(refs) > 4:
+        efficiency_ref, own_ref, *refs, binned_ref, left_ref, left_high_ref = refs
+        rows = efficiency_ref.shape[0]
+        firsts = gather_left([own_ref], efficiency_ref, left_ref, left_high_ref, orders, cycles_here, (0,))
+        own = True
+    else:
+        own = False
+    high_ref, low_ref, table_high_ref, table_low_ref = refs
+
+    def step(start):
+        lanes = pl.ds(start, TILE)
+        high, low = split(window_ref[:, lanes])
+        high_ref[:, lanes], low_ref[:, lanes] = high, low
+        table_high_ref[:, :, lanes], table_low_ref[:, :, lanes] = split(legendre_ref[:, :, lanes])
+        if own:
+            binned = add_cycles(
+                [jnp.zeros((rows, TILE), jnp.float32)] * orders, left_ref[...], left_high_ref[...],
+                high, low, legendre_ref, firsts, lanes, orders, rows,
+            )
+            for m in range(orders):
+                binned_ref[pl.ds(m * rows, rows), lanes] = binned[m]
+
+    each_tile(legendre_ref.shape[2], own, step)
+
+
+def more_kernel(
+    efficiency_ref, legendre_ref, high_ref, low_ref, binned_in, modes_ref, binned_ref, left_ref, left_high_ref,
+    *, orders, cycles_here, offset,
 ):
-    *modes_refs, binned_ref, left_ref, left_high_ref = refs
     rows = efficiency_ref.shape[0]
-    firsts = gather_left(modes_refs, efficiency_ref, left_ref, left_high_ref, orders, cycles_here, offsets)
+    firsts = gather_left([modes_ref], efficiency_ref, left_ref, left_high_ref, orders, cycles_here, (offset,))
 
     def step(start):
         lanes = pl.ds(start, TILE)
         binned = add_cycles(
-            [jnp.zeros((rows, TILE), jnp.float32)] * orders, left_ref[...], left_high_ref[...],
+            [binned_in[pl.ds(m * rows, rows), lanes] for m in range(orders)], left_ref[...], left_high_ref[...],
             high_ref[:, lanes], low_ref[:, lanes], legendre_ref, firsts, lanes, orders, rows,
         )
         for m in range(orders):
@@ -200,46 +221,60 @@
 
     kappa = own(0) + jnp.where(table == KAPPA_HIGH, own(1), 0.0)
     value = jnp.where(table < PLUS, kappa, own(2))
-    for b in range(bins):
-        for z in range(bands):
-            for c in range(2):
-                out_ref[b * bands + z, c : c + 1, :] = value[c * bins + b : c * bins + b + 1]
+    count = 4 * columns // LANES
+    slot = iota((rows, LANES), 1) % cycles // cycles_here
+    shifted = {}
+    for z in range(bands):
+        halves = []
+        for c in range(2):
+            half = jnp.zeros((rows, LANES), jnp.float32)
+            for v in range(count):
+                at = c * count + v
+                shift = (at - z) * cycles_here % LANES
+                if (v, shift) not in shifted:
+                    part = value[:, v * LANES : (v + 1) * LANES]
+                    shifted[v, shift] = pltpu.roll(part, shift, 1) if shift else part
+                half = jnp.where(slot == at, shifted[v, shift], half)
+            halves.append(half)
+        row = jnp.where(slot[:bins] < count, halves[0][:bins], halves[1][bins:])
+        for b in range(bins):
+            out_ref[b * bands + z] = row[b : b + 1]
 
 
 def unpack_kernel(got_ref, out_ref, *, bands, orders, cycles_here):
-    width = got_ref.shape[2]
     groups = got_ref.shape[0] // bands
     cycles = bands * cycles_here
     columns = orders * cycles
-    own_order = iota((orders, width), 1) % columns // cycles == iota((orders, width), 0)
-    shape = (3 * cycles_here * 2, width)
+    count = 4 * columns // LANES
+
+    def origin(lane):
+        slot = lane % cycles // cycles_here
+        source = slot % count * LANES + lane // cycles * cycles
+        return slot // count, source // columns, source % columns // cycles
+
+    shape = (orders, LANES)
+    own_order = origin(iota(shape, 1))[2] == iota(shape, 0)
+    values = []
+    for z in range(bands):
+        total = got_ref[z]
+        for p in range(1, groups):
+            total = total + got_ref[p * bands + z]
+        values.append(jnp.where(own_order, jnp.broadcast_to(total, shape), 0.0))
+    shape = (3 * cycles_here * 2, LANES)
     row, lane = iota(shape, 0), iota(shape, 1)
     field, cycle, part = row // (2 * cycles_here), row // 2 % cycles_here, row % 2
-    table = lane // columns
-    here = lane % cycles == lax.axis_index("band") * cycles_here + cycle
-    total = [got_ref[z] for z in range(bands)]
-    for p in range(1, groups):
-        total = [total[z] + got_ref[p * bands + z] for z in range(bands)]
-    maps = jnp.zeros((3 * cycles_here * 2, bands * orders), jnp.float32)
-    for c in range(2):
-        values = jnp.concatenate(
-            [
-                jnp.where(own_order, jnp.broadcast_to(total[z][c : c + 1], (orders, width)), 0.0)
-                for z in range(bands)
-            ],
-            0,
-        )
-        same = jnp.where(part == c, 1.0, 0.0)
-        other = jnp.where(part == c, 0.0, 1.0 if c == 0 else -1.0)
-        pick = jnp.where(
-            field == 0,
-            jnp.where(table <= KAPPA_LOW, same, 0.0),
-            jnp.where(field == 1, jnp.where(table == PLUS, same, 0.0), jnp.where(table == MINUS, other, 0.0)),
-        )
-        maps = maps + lax.dot_general(
-            jnp.where(here, pick, 0.0), values, (((1,), (1,)), ((), ())),
-            precision=lax.Precision.HIGHEST, preferred_element_type=jnp.float32,
-        )
+    lane_part, table, _ = origin(lane)
+    same = jnp.where(lane_part == part, 1.0, 0.0)
+    other = jnp.where(lane_part == part, 0.0, jnp.where(part == 0, -1.0, 1.0))
+    pick = jnp.where(
+        field == 0,
+        jnp.where(table <= KAPPA_LOW, same, 0.0),
+        jnp.where(field == 1, jnp.where(table == PLUS, same, 0.0), jnp.where(table == MINUS, other, 0.0)),
+    )
+    maps = lax.dot_general(
+        jnp.where(lane % cycles_here == cycle, pick, 0.0), jnp.concatenate(values, 0), (((1,), (1,)), ((), ())),
+        precision=lax.Precision.HIGHEST, preferred_element_type=jnp.float32,
+    )
     for i in range(3 * cycles_here):
         out_ref[i] = maps[2 * i : 2 * i + 2]
 
@@ -252,7 +287,7 @@
     shells, cycles_here, _, orders_all = cycle_modes.shape
     orders, cycles, degrees = legendre.shape
     bins = source_shell.shape[0]
-    assert bins == shell_parts
+    assert bins == shell_parts and 8 * orders * cycles_here == LANES
     offsets = (2, 3, 1) if bands == 4 else ()
     rows = 2 * bins
     columns = 4 * orders * cycles
@@ -269,26 +304,29 @@
     block_shape = (cycles_here, 2 * orders, shells)
     out_shape = [shaped(*block_shape)] * bands if offsets else [shaped(bands, *block_shape)]
     out_shape = [*out_shape, shaped(rows, shells)]
+    sources = (
+        cycle_modes.transpose(1, 2, 3, 0), cycle_weight.reshape(1, cycles_here),
+        source_shell.reshape(1, bins), lensing.reshape(1, shells),
+    )
+    sources = pl.pallas_call(
+        load_kernel,
+        in_specs=[HBM] * 4,
+        out_specs=[VMEM] * 4,
+        out_shape=[shaped(*x.shape, dtype=x.dtype) for x in sources],
+        scratch_shapes=[pltpu.SemaphoreType.DMA((4,))],
+        compiler_params=PARAMS,
+        name="load",
+    )(*map(keep, sources))
     *blocks, efficiency = pl.pallas_call(
         functools.partial(pack_kernel, bands=bands, orders=orders, bins=bins, offsets=offsets),
-        in_specs=[HBM] * 4,
+        in_specs=[VMEM] * 4,
         out_specs=[VMEM] * len(out_shape),
         out_shape=out_shape,
-        scratch_shapes=[
-            pltpu.VMEM((bands, *block_shape), jnp.float32),
-            pltpu.VMEM((cycles_here, 2, orders_all, shells), jnp.float32),
-            pltpu.VMEM((1, cycles_here), jnp.float32),
-            pltpu.VMEM((1, bins), jnp.int32),
-            pltpu.VMEM((1, shells), jnp.float32),
-            pltpu.SemaphoreType.DMA((4,)),
-        ],
+        scratch_shapes=[pltpu.VMEM((bands, *block_shape), jnp.float32)],
         compiler_params=PARAMS,
         cost_estimate=pl.CostEstimate(flops=10**10, bytes_accessed=2**17, transcendentals=0),
         name="pack",
-    )(
-        keep(cycle_modes.transpose(1, 2, 3, 0)), keep(cycle_weight.reshape(1, cycles_here)),
-        keep(source_shell.reshape(1, bins)), keep(lensing.reshape(1, shells)),
-    )
+    )(*sources)
     if offsets:
         own, *sends = blocks
         got = [
@@ -298,39 +336,42 @@
     else:
         got = [lax.all_to_all(blocks[0], "band", split_axis=0, concat_axis=0, tiled=True)]
     half = jnp.bfloat16
-    high, low, table_high, table_low = pl.pallas_call(
-        prepare_kernel,
-        in_specs=[VMEM] * 2,
-        out_specs=[VMEM] * 4,
-        out_shape=[shaped(shells, degrees, dtype=half)] * 2 + [shaped(orders, cycles, degrees, dtype=half)] * 2,
+    tables = [shaped(shells, degrees, dtype=half)] * 2 + [shaped(orders, cycles, degrees, dtype=half)] * 2
+    binned_shape = shaped(orders * rows, degrees)
+    arguments = [window, legendre, spin_plus, spin_minus]
+    if offsets:
+        tables.append(binned_shape)
+        arguments += [efficiency, own]
+    high, low, table_high, table_low, *binned = pl.pallas_call(
+        functools.partial(prepare_kernel, orders=orders, cycles_here=cycles_here),
+        in_specs=[VMEM] * len(arguments),
+        out_specs=[VMEM] * len(tables),
+        out_shape=tables,
+        scratch_shapes=left_scratch(1) if offsets else [],
         compiler_params=PARAMS,
         name="prepare",
-    )(window, legendre)
-    operands = [efficiency, legendre, high, low, table_high, table_low, spin_plus, spin_minus]
-    last = got
-    if offsets:
-        last = got[1:]
-        operands.append(
+    )(*arguments)
+    for k, block in zip(offsets[:-1], got):
+        binned = [
             pl.pallas_call(
-                functools.partial(
-                    first_kernel, orders=orders, cycles_here=cycles_here, offsets=(0, offsets[0])
-                ),
+                functools.partial(more_kernel, orders=orders, cycles_here=cycles_here, offset=k),
                 in_specs=[VMEM] * 6,
                 out_specs=VMEM,
-                out_shape=shaped(orders * rows, degrees),
-                scratch_shapes=left_scratch(2),
+                out_shape=binned_shape,
+                scratch_shapes=left_scratch(1),
                 compiler_params=PARAMS,
-                name="first",
-            )(efficiency, legendre, high, low, own, got[0])
-        )
-    operands += last
+                name="more",
+            )(efficiency, legendre, high, low, *binned, block)
+        ]
+    last = got[-1:]
+    operands = [efficiency, legendre, high, low, table_high, table_low, spin_plus, spin_minus, *binned, *last]
     maps = pl.pallas_call(
         functools.partial(
-            maps_kernel, bands=bands, orders=orders, cycles_here=cycles_here, offsets=offsets[1:]
+            maps_kernel, bands=bands, orders=orders, cycles_here=cycles_here, offsets=offsets[-1:]
         ),
         in_specs=[VMEM] * len(operands),
         out_specs=VMEM,
-        out_shape=shaped(bins * bands, 2, columns),
+        out_shape=shaped(bins * bands, 1, LANES),
         scratch_shapes=[
             *left_scratch(len(last) if offsets else bands),
             pltpu.VMEM((3 * orders * rows, columns), jnp.float32),

time: 24.8 us -> 23.8 us (0.960)
  blocking collectives: 10.6 us -> 9.85 us
  Pallas kernels: 5.99 us -> 5.65 us
    pallas_call x2 -> x4, Pallas kernels: 1.74 us -> 3.23 us  [the longest x2 1.47 us: on_device(): pl.pallas_call(functools.partial(more_kernel, orders=orders, cycles_here=...]
    pallas_call x1, Pallas kernels: 1.12 us -> 0.1 us  [on_device(): pl.pallas_call(functools.partial(pack_kernel, bands=bands, orders=orders,...]
    pallas_call x1, Pallas kernels: 2.32 us -> 1.54 us  [on_device(): pl.pallas_call(functools.partial(maps_kernel, bands=bands, orders=orders,...]
    all_to_all x1, blocking collectives: 10.6 us -> 9.85 us  [on_device(): lax.all_to_all(maps, ('shell', 'band'), split_axis=0, concat_axis=0, tile...]
  transfers between devices with their start and end apart: 3 -> 3, of which waited for: 1 -> 1; matrix products, arithmetic and copies ran while one was open for 0% -> 0% of each run, Pallas kernels for 7% -> 10%
where the time goes in v4:
time: 23.8 us; the launch traced here: 23.6 us
  blocking collectives  9.85 us (41%)
  starting transfers between devices  5.71 us (24%)
  Pallas kernels  5.65 us (24%)
  waiting for transfers between devices  2.3 us (10%)
    all_to_all x1, blocking collectives, on_device(): lax.all_to_all(maps, ('shell', 'band'), split_axis=0, concat_axis=0, tile...  9.85 us
    ppermute x3, starting transfers between devices, on_device(): lax.ppermute(send, 'band', [(z, z ^ k) for z in range(bands)])  5.71 us
    ppermute x3, waiting for transfers between devices, on_device(): lax.ppermute(send, 'band', [(z, z ^ k) for z in range(bands)])  2.3 us
    pallas_call x1, Pallas kernels, on_device(): pl.pallas_call(functools.partial(maps_kernel, bands=bands, orders=orders,...  1.54 us
    pallas_call x2, Pallas kernels, on_device(): pl.pallas_call(functools.partial(more_kernel, orders=orders, cycles_here=...  1.47 us
    pallas_call x1, Pallas kernels, on_device(): pl.pallas_call(load_kernel, in_specs=[HBM] * 4, out_specs=[VMEM] * 4, out...  0.88 us
    pallas_call x1, Pallas kernels, on_device(): pl.pallas_call(functools.partial(prepare_kernel, orders=orders, cycles_he...  0.88 us
    pallas_call x1, Pallas kernels, on_device(): pl.pallas_call(functools.partial(unpack_kernel, bands=bands, orders=order...  0.78 us
  transfers between devices with their start and end apart: 3, of which 1 were waited for; matrix products, arithmetic and copies ran while one was open for 0% of the time, Pallas kernels for 10%

profile of v4, /device:TPU:0, one launch (start us, length us, event | category | flops | bytes accessed | tf_op | source)
XLA Modules:
  0.0 23.6 jit_solution(8437436002231672862)
XLA Ops:
  0.0 0.9 %load.1 = (f32[4,2,16,128]{3,2,1,0:T(8,128)S(1)}, f32[1,4]{1,0:T(1,128)S(1)}, s32[1,4]{1,0:T(1,128)S(1)}, f32[1,128]{1,0:T(1,128)S(1)}) custom-call(f32[4,2,16,128]{3,2,1,0:T(8,128)} %bitcast.5, f32[1,4]{1,0:T(1,128)} %bitcast.6, s32[1,4]{1,0:T(1,128)} %bitcast.7, f32[1,128]{1,0:T(1,128)} %bitcast.8), custom_call_target="tpu_custom_call" | custom-call | tf_op jit(solution)/shard_map/load/pallas_call | solution.py:311
  0.9 0.0 copy-start
  0.9 0.0 copy-start.1
  0.9 0.0 copy-start.2
  0.9 0.0 copy-start.3
  0.9 0.1 pack.1
  1.0 4.1 %collective-permute-start = (f32[4,8,128]{2,1,0:T(8,128)S(1)}, f32[4,8,128]{2,1,0:T(8,128)S(1)}, u32[]{:S(2)}, u32[]{:S(2)}) collective-permute-start(f32[4,8,128]{2,1,0:T(8,128)S(1)} %get-tuple-element.30), channel_id=1, source_target_pairs={{0,2},{1,3},{2,0},{3,1},{4,6},{5,7},{6,4},{7,5},{8,10},{9,11},{10,... | collective-permute-start | bytes 49160 | tf_op jit(solution)/shard_map/ppermute | solution.py:333
  5.2 1.3 %collective-permute-start.1 = (f32[4,8,128]{2,1,0:T(8,128)S(1)}, f32[4,8,128]{2,1,0:T(8,128)S(1)}, u32[]{:S(2)}, u32[]{:S(2)}) collective-permute-start(f32[4,8,128]{2,1,0:T(8,128)S(1)} %get-tuple-element.31), channel_id=1, source_target_pairs={{0,3},{1,2},{2,1},{3,0},{4,7},{5,6},{6,5},{7,4},{8,11},{9,10},{10,... | collective-permute-start | bytes 49160 | tf_op jit(solution)/shard_map/ppermute | solution.py:333
  6.5 0.2 collective-permute-start.2
  6.7 0.0 copy-done
  6.7 0.0 copy-done.1
  6.7 0.0 copy-done.2
  6.7 0.0 copy-done.3
  6.8 0.9 %prepare.1 = (bf16[128,4096]{1,0:T(8,128)(2,1)S(1)}, bf16[128,4096]{1,0:T(8,128)(2,1)S(1)}, bf16[4,16,4096]{2,1,0:T(8,128)(2,1)S(1)}, bf16[4,16,4096]{2,1,0:T(8,128)(2,1)S(1)}, f32[32,4096]{1,0:T(8,128)S(1)}) custom-call(f32[128,4096]{1,0:T(8,128)S(1)} %copy-done.3, f32[4,16,4096]{2,1,0:T(8,128)S(1)} %copy-done, bf16[4,16,4096]{2,1,0:T(8,128)(2,1)S(1)} %copy-done.1, ...), custom_call_target="tpu_custom_call" | custom-call | tf_op jit(solution)/shard_map/prepare/pallas_call | solution.py:345
  7.6 0.0 collective-permute-done.modes_ref
  7.7 0.7 %more.2.binned_in = f32[32,4096]{1,0:T(8,128)S(1)} custom-call(f32[8,128]{1,0:T(8,128)S(1)} %get-tuple-element.23.refs_0_.efficiency_ref, f32[4,16,4096]{2,1,0:T(8,128)S(1)} %copy-done, bf16[128,4096]{1,0:T(8,128)(2,1)S(1)} %get-tuple-element.25.high_ref, bf16[128,4096]{1,0:T(8,128)(2,1)S(1)} %get-tuple-element.26.low_ref, ...), custom_call_target="tpu_custom_call" | custom-call | tf_op jit(solution)/shard_map/more/pallas_call | solution.py:356
  8.4 2.3 %collective-permute-done.1.modes_ref = f32[4,8,128]{2,1,0:T(8,128)S(1)} collective-permute-done((f32[4,8,128]{2,1,0:T(8,128)S(1)}, f32[4,8,128]{2,1,0:T(8,128)S(1)}, u32[]{:S(2)}, u32[]{:S(2)}) %collective-permute-start.1) | collective-permute-done | bytes 16416 | tf_op jit(solution)/shard_map/ppermute | solution.py:333
  10.7 0.7 %more.3.refs_0_ = f32[32,4096]{1,0:T(8,128)S(1)} custom-call(f32[8,128]{1,0:T(8,128)S(1)} %get-tuple-element.23.refs_0_.efficiency_ref, f32[4,16,4096]{2,1,0:T(8,128)S(1)} %copy-done, bf16[128,4096]{1,0:T(8,128)(2,1)S(1)} %get-tuple-element.25.high_ref, bf16[128,4096]{1,0:T(8,128)(2,1)S(1)} %get-tuple-element.26.low_ref, f32[32,4096]{1,0:T(8,128)S(1)} %more.2.binned_in, ...), custom_call_target="tpu_custom_call" | custom-call | tf_op jit(solution)/shard_map/more/pallas_call | solution.py:356
  11.4 0.0 collective-permute-done.2.refs_1_
  11.4 1.5 %maps.1 = f32[16,1,128]{2,1,0:T(1,128)S(1)} custom-call(f32[8,128]{1,0:T(8,128)S(1)} %get-tuple-element.23.refs_0_.efficiency_ref, f32[4,16,4096]{2,1,0:T(8,128)S(1)} %copy-done, bf16[128,4096]{1,0:T(8,128)(2,1)S(1)} %get-tuple-element.25.high_ref, bf16[128,4096]{1,0:T(8,128)(2,1)S(1)} %get-tuple-element.26.low_ref, ...), custom_call_target="tpu_custom_call" | custom-call | tf_op jit(solution)/shard_map/maps/pallas_call | solution.py:368
  13.0 9.9 %all_to_all.5.got_ref = f32[16,1,128]{2,1,0:T(1,128)S(1)} all-to-all(f32[16,1,128]{2,1,0:T(1,128)S(1)} %maps.1), channel_id=1, replica_groups=mesh['cosmo'=2,'shell'=4,'band'=4] {'shell','band'}, dimensions={0} | all-to-all | bytes 16384 | tf_op jit(solution)/shard_map/all_to_all | solution.py:382
  22.8 0.8 %unpack.1 = f32[12,2,16]{2,1,0:T(2,128)} custom-call(f32[16,1,128]{2,1,0:T(1,128)S(1)} %all_to_all.5.got_ref), custom_call_target="tpu_custom_call" | custom-call | tf_op jit(solution)/shard_map/unpack/pallas_call | solution.py:383
Async XLA Ops:
  0.9 5.9 %copy-start = (f32[4,16,4096]{2,1,0:T(8,128)S(1)}, f32[4,16,4096]{2,1,0:T(8,128)}, u32[]{:S(2)}) copy-start(f32[4,16,4096]{2,1,0:T(8,128)} %legendre_ref.7) | copy-start | bytes 3145732
  0.9 5.8 %copy-start.1 = (bf16[4,16,4096]{2,1,0:T(8,128)(2,1)S(1)}, bf16[4,16,4096]{2,1,0:T(8,128)(2,1)}, u32[]{:S(2)}) copy-start(bf16[4,16,4096]{2,1,0:T(8,128)(2,1)} %plus_ref.3) | copy-start | bytes 1572868
  0.9 5.8 %copy-start.2 = (bf16[4,16,4096]{2,1,0:T(8,128)(2,1)S(1)}, bf16[4,16,4096]{2,1,0:T(8,128)(2,1)}, u32[]{:S(2)}) copy-start(bf16[4,16,4096]{2,1,0:T(8,128)(2,1)} %minus_ref.3) | copy-start | bytes 1572868
  0.9 5.8 %copy-start.3 = (f32[128,4096]{1,0:T(8,128)S(1)}, f32[128,4096]{1,0:T(8,128)}, u32[]{:S(2)}) copy-start(f32[128,4096]{1,0:T(8,128)} %window_ref.1) | copy-start | bytes 6291460
  1.0 6.6 %collective-permute-start = (f32[4,8,128]{2,1,0:T(8,128)S(1)}, f32[4,8,128]{2,1,0:T(8,128)S(1)}, u32[]{:S(2)}, u32[]{:S(2)}) collective-permute-start(f32[4,8,128]{2,1,0:T(8,128)S(1)} %get-tuple-element.30), channel_id=1, source_target_pairs={{0,2},{1,3},{2,0},{3,1},{4,6},{5,7},{6,4},{7,5},{8,10},{9,11},{10,... | collective-permute-start | bytes 49160 | tf_op jit(solution)/shard_map/ppermute | solution.py:333
  5.2 5.5 %collective-permute-start.1 = (f32[4,8,128]{2,1,0:T(8,128)S(1)}, f32[4,8,128]{2,1,0:T(8,128)S(1)}, u32[]{:S(2)}, u32[]{:S(2)}) collective-permute-start(f32[4,8,128]{2,1,0:T(8,128)S(1)} %get-tuple-element.31), channel_id=1, source_target_pairs={{0,3},{1,2},{2,1},{3,0},{4,7},{5,6},{6,5},{7,4},{8,11},{9,10},{10,... | collective-permute-start | bytes 49160 | tf_op jit(solution)/shard_map/ppermute | solution.py:333
  6.5 4.9 %collective-permute-start.2 = (f32[4,8,128]{2,1,0:T(8,128)S(1)}, f32[4,8,128]{2,1,0:T(8,128)S(1)}, u32[]{:S(2)}, u32[]{:S(2)}) collective-permute-start(f32[4,8,128]{2,1,0:T(8,128)S(1)} %get-tuple-element.32), channel_id=1, source_target_pairs={{0,1},{1,0},{2,3},{3,2},{4,5},{5,4},{6,7},{7,6},{8,9},{9,8},{10,11... | collective-permute-start | bytes 49160 | tf_op jit(solution)/shard_map/ppermute | solution.py:333

commit v5 on v4

--- a/solution.py
+++ b/solution.py
@@ -8,6 +8,7 @@
 from jax.sharding import PartitionSpec as P
 
 TILE = 256
+GROUP = 16
 LANES = 128
 VMEM = pl.BlockSpec(memory_space=pltpu.VMEM)
 HBM = pl.BlockSpec(memory_space=pltpu.HBM)
@@ -81,9 +82,12 @@
     return jnp.concatenate([high, low], 1), high
 
 
-def add_cycles(binned, left, left_high, high, low, legendre_ref, firsts, lanes, orders, rows):
+def multiply(left, left_high, high, low):
     product = jnp.dot(left, jnp.concatenate([high, high], 0), preferred_element_type=jnp.float32)
-    product = product + jnp.dot(left_high, low, preferred_element_type=jnp.float32)
+    return product + jnp.dot(left_high, low, preferred_element_type=jnp.float32)
+
+
+def add_cycles(binned, product, legendre_ref, firsts, lanes, orders, rows):
     out = []
     at = 0
     for m in range(orders):
@@ -96,12 +100,12 @@
     return out
 
 
-def each_tile(degrees, unroll, step):
+def each_tile(degrees, unroll, step, size=TILE):
     if unroll:
-        for start in range(0, degrees, TILE):
+        for start in range(0, degrees, size):
             step(start)
     else:
-        pl.loop(0, degrees // TILE)(lambda i: step(pl.multiple_of(i * TILE, TILE)))
+        pl.loop(0, degrees // size)(lambda i: step(pl.multiple_of(i * size, size)))
 
 
 def gather_left(modes_refs, efficiency_ref, left_ref, left_high_ref, orders, cycles_here, offsets):
@@ -120,24 +124,33 @@
 
 
 def prepare_kernel(window_ref, legendre_ref, plus_ref, minus_ref, *refs, orders, cycles_here):
-    if len(refs) > 4:
+    if len(refs) > 3:
         efficiency_ref, own_ref, *refs, binned_ref, left_ref, left_high_ref = refs
         rows = efficiency_ref.shape[0]
         firsts = gather_left([own_ref], efficiency_ref, left_ref, left_high_ref, orders, cycles_here, (0,))
         own = True
     else:
         own = False
-    high_ref, low_ref, table_high_ref, table_low_ref = refs
+    high_ref, low_ref, tables_ref = refs
+    columns = legendre_ref.shape[0] * legendre_ref.shape[1]
+    same = jnp.where(iota((TILE, TILE), 0) == iota((TILE, TILE), 1), 1.0, 0.0).astype(jnp.bfloat16)
 
     def step(start):
         lanes = pl.ds(start, TILE)
         high, low = split(window_ref[:, lanes])
         high_ref[:, lanes], low_ref[:, lanes] = high, low
-        table_high_ref[:, :, lanes], table_low_ref[:, :, lanes] = split(legendre_ref[:, :, lanes])
+        tables = [
+            *split(legendre_ref[:, :, lanes].reshape(columns, TILE)),
+            plus_ref[:, :, lanes].reshape(columns, TILE),
+            minus_ref[:, :, lanes].reshape(columns, TILE),
+        ]
+        tables_ref[lanes, :] = lax.dot_general(
+            same, jnp.concatenate(tables, 0), (((1,), (1,)), ((), ())), preferred_element_type=jnp.float32,
+        ).astype(jnp.bfloat16)
         if own:
             binned = add_cycles(
-                [jnp.zeros((rows, TILE), jnp.float32)] * orders, left_ref[...], left_high_ref[...],
-                high, low, legendre_ref, firsts, lanes, orders, rows,
+                [jnp.zeros((rows, TILE), jnp.float32)] * orders,
+                multiply(left_ref[...], left_high_ref[...], high, low), legendre_ref, firsts, lanes, orders, rows,
             )
             for m in range(orders):
                 binned_ref[pl.ds(m * rows, rows), lanes] = binned[m]
@@ -155,8 +168,9 @@
     def step(start):
         lanes = pl.ds(start, TILE)
         binned = add_cycles(
-            [binned_in[pl.ds(m * rows, rows), lanes] for m in range(orders)], left_ref[...], left_high_ref[...],
-            high_ref[:, lanes], low_ref[:, lanes], legendre_ref, firsts, lanes, orders, rows,
+            [binned_in[pl.ds(m * rows, rows), lanes] for m in range(orders)],
+            multiply(left_ref[...], left_high_ref[...], high_ref[:, lanes], low_ref[:, lanes]),
+            legendre_ref, firsts, lanes, orders, rows,
         )
         for m in range(orders):
             binned_ref[pl.ds(m * rows, rows), lanes] = binned[m]
@@ -165,7 +179,7 @@
 
 
 def maps_kernel(
-    efficiency_ref, legendre_ref, high_ref, low_ref, table_high_ref, table_low_ref, plus_ref, minus_ref, *refs,
+    efficiency_ref, legendre_ref, high_ref, low_ref, tables_ref, *refs,
     bands, orders, cycles_here, offsets,
 ):
     if offsets:
@@ -178,16 +192,15 @@
     firsts = gather_left(modes_refs, efficiency_ref, left_ref, left_high_ref, orders, cycles_here, offsets)
     sums_ref[...] = jnp.zeros(sums_ref.shape, jnp.float32)
 
-    def step(start):
+    group = GROUP if offsets else 2
+
+    def coefficients(start, product):
         lanes = pl.ds(start, TILE)
         if offsets:
             binned = [binned_ref[pl.ds(m * rows, rows), lanes] for m in range(orders)]
         else:
             binned = [jnp.zeros((rows, TILE), jnp.float32)] * orders
-        binned = add_cycles(
-            binned, left_ref[...], left_high_ref[...], high_ref[:, lanes], low_ref[:, lanes],
-            legendre_ref, firsts, lanes, orders, rows,
-        )
+        binned = add_cycles(binned, product, legendre_ref, firsts, lanes, orders, rows)
         binned = jnp.concatenate(binned, 0)
         degree = (start + iota((rows, TILE), 1)).astype(jnp.float32)
         ratio = jnp.where(
@@ -197,17 +210,22 @@
         )
         shear = (-jnp.concatenate([ratio] * orders, 0) * binned).astype(jnp.bfloat16)
         high, low = split(binned)
-        tables = [
-            ref[:, :, lanes].reshape(columns, TILE)
-            for ref in (table_high_ref, table_low_ref, plus_ref, minus_ref)
-        ]
-        sums_ref[...] += lax.dot_general(
-            jnp.concatenate([high, low, shear], 0), jnp.concatenate(tables, 0),
-            (((1,), (1,)), ((), ())),
-            preferred_element_type=jnp.float32,
-        )
-
-    each_tile(legendre_ref.shape[2], bool(offsets), step)
+        return jnp.concatenate([high, low, shear], 0)
+
+    def step(start):
+        starts = [start + i * TILE for i in range(group)]
+        spans = [pl.ds(at, TILE) for at in starts]
+        products = [
+            multiply(left_ref[...], left_high_ref[...], high_ref[:, lanes], low_ref[:, lanes]) for lanes in spans
+        ]
+        lefts = [coefficients(*pair) for pair in zip(starts, products)]
+        parts = [
+            jnp.dot(left, tables_ref[lanes, :], preferred_element_type=jnp.float32)
+            for left, lanes in zip(lefts, spans)
+        ]
+        sums_ref[...] += sum(parts[1:], parts[0])
+
+    each_tile(legendre_ref.shape[2], bool(offsets), step, group * TILE)
 
     lane = iota((rows, 4 * columns), 1)
     table = lane // columns
@@ -336,13 +354,13 @@
     else:
         got = [lax.all_to_all(blocks[0], "band", split_axis=0, concat_axis=0, tiled=True)]
     half = jnp.bfloat16
-    tables = [shaped(shells, degrees, dtype=half)] * 2 + [shaped(orders, cycles, degrees, dtype=half)] * 2
+    tables = [shaped(shells, degrees, dtype=half)] * 2 + [shaped(degrees, columns, dtype=half)]
     binned_shape = shaped(orders * rows, degrees)
     arguments = [window, legendre, spin_plus, spin_minus]
     if offsets:
         tables.append(binned_shape)
         arguments += [efficiency, own]
-    high, low, table_high, table_low, *binned = pl.pallas_call(
+    high, low, turned, *binned = pl.pallas_call(
         functools.partial(prepare_kernel, orders=orders, cycles_here=cycles_here),
         in_specs=[VMEM] * len(arguments),
         out_specs=[VMEM] * len(tables),
@@ -364,7 +382,7 @@
             )(efficiency, legendre, high, low, *binned, block)
         ]
     last = got[-1:]
-    operands = [efficiency, legendre, high, low, table_high, table_low, spin_plus, spin_minus, *binned, *last]
+    operands = [efficiency, legendre, high, low, turned, *binned, *last]
     maps = pl.pallas_call(
         functools.partial(
             maps_kernel, bands=bands, orders=orders, cycles_here=cycles_here, offsets=offsets[-1:]

time: 23.8 us -> 23.6 us (level)
  waiting for transfers between devices: 2.3 us -> 1.81 us
    pallas_call x1, Pallas kernels: 0.88 us -> 1.37 us  [on_device(): pl.pallas_call(functools.partial(prepare_kernel, orders=orders, cycles_he...]
    ppermute x3, waiting for transfers between devices: 2.3 us -> 1.81 us  [on_device(): lax.ppermute(send, 'band', [(z, z ^ k) for z in range(bands)])]
    pallas_call x1, Pallas kernels: 1.54 us -> 1.29 us  [on_device(): pl.pallas_call(functools.partial(maps_kernel, bands=bands, orders=orders,...]
  transfers between devices with their start and end apart: 3 -> 3, of which waited for: 1 -> 1; matrix products, arithmetic and copies ran while one was open for 0% -> 0% of each run, Pallas kernels for 10% -> 12%
where the time goes in v5:
time: 23.6 us; the launch traced here: 23.4 us
  blocking collectives  9.87 us (42%)
  Pallas kernels  5.88 us (25%)
  starting transfers between devices  5.71 us (24%)
  waiting for transfers between devices  1.81 us (8%)
    all_to_all x1, blocking collectives, on_device(): lax.all_to_all(maps, ('shell', 'band'), split_axis=0, concat_axis=0, tile...  9.87 us
    ppermute x3, starting transfers between devices, on_device(): lax.ppermute(send, 'band', [(z, z ^ k) for z in range(bands)])  5.71 us
    ppermute x3, waiting for transfers between devices, on_device(): lax.ppermute(send, 'band', [(z, z ^ k) for z in range(bands)])  1.81 us
    pallas_call x2, Pallas kernels, on_device(): pl.pallas_call(functools.partial(more_kernel, orders=orders, cycles_here=...  1.46 us
    pallas_call x1, Pallas kernels, on_device(): pl.pallas_call(functools.partial(prepare_kernel, orders=orders, cycles_he...  1.37 us
    pallas_call x1, Pallas kernels, on_device(): pl.pallas_call(functools.partial(maps_kernel, bands=bands, orders=orders,...  1.29 us
    pallas_call x1, Pallas kernels, on_device(): pl.pallas_call(load_kernel, in_specs=[HBM] * 4, out_specs=[VMEM] * 4, out...  0.88 us
    pallas_call x1, Pallas kernels, on_device(): pl.pallas_call(functools.partial(unpack_kernel, bands=bands, orders=order...  0.78 us
  transfers between devices with their start and end apart: 3, of which 1 were waited for; matrix products, arithmetic and copies ran while one was open for 0% of the time, Pallas kernels for 12%

profile of v5, /device:TPU:0, one launch (start us, length us, event | category | flops | bytes accessed | tf_op | source)
XLA Modules:
  0.0 23.4 jit_solution(17507180166721110258)
XLA Ops:
  0.0 0.9 %load.1 = (f32[4,2,16,128]{3,2,1,0:T(8,128)S(1)}, f32[1,4]{1,0:T(1,128)S(1)}, s32[1,4]{1,0:T(1,128)S(1)}, f32[1,128]{1,0:T(1,128)S(1)}) custom-call(f32[4,2,16,128]{3,2,1,0:T(8,128)} %bitcast.5, f32[1,4]{1,0:T(1,128)} %bitcast.6, s32[1,4]{1,0:T(1,128)} %bitcast.7, f32[1,128]{1,0:T(1,128)} %bitcast.8), custom_call_target="tpu_custom_call" | custom-call | tf_op jit(solution)/shard_map/load/pallas_call | solution.py:329
  0.9 0.0 copy-start
  0.9 0.0 copy-start.1
  0.9 0.0 copy-start.2
  0.9 0.0 copy-start.3
  0.9 0.1 pack.1
  1.0 4.1 %collective-permute-start = (f32[4,8,128]{2,1,0:T(8,128)S(1)}, f32[4,8,128]{2,1,0:T(8,128)S(1)}, u32[]{:S(2)}, u32[]{:S(2)}) collective-permute-start(f32[4,8,128]{2,1,0:T(8,128)S(1)} %get-tuple-element.28), channel_id=1, source_target_pairs={{0,2},{1,3},{2,0},{3,1},{4,6},{5,7},{6,4},{7,5},{8,10},{9,11},{10,... | collective-permute-start | bytes 49160 | tf_op jit(solution)/shard_map/ppermute | solution.py:351
  5.2 1.3 %collective-permute-start.1 = (f32[4,8,128]{2,1,0:T(8,128)S(1)}, f32[4,8,128]{2,1,0:T(8,128)S(1)}, u32[]{:S(2)}, u32[]{:S(2)}) collective-permute-start(f32[4,8,128]{2,1,0:T(8,128)S(1)} %get-tuple-element.29), channel_id=1, source_target_pairs={{0,3},{1,2},{2,1},{3,0},{4,7},{5,6},{6,5},{7,4},{8,11},{9,10},{10,... | collective-permute-start | bytes 49160 | tf_op jit(solution)/shard_map/ppermute | solution.py:351
  6.5 0.2 collective-permute-start.2
  6.7 0.0 copy-done
  6.7 0.0 copy-done.1
  6.7 0.0 copy-done.2
  6.7 0.0 copy-done.3
  6.8 1.4 %prepare.1 = (bf16[128,4096]{1,0:T(8,128)(2,1)S(1)}, bf16[128,4096]{1,0:T(8,128)(2,1)S(1)}, bf16[4096,256]{1,0:T(8,128)(2,1)S(1)}, f32[32,4096]{1,0:T(8,128)S(1)}) custom-call(f32[128,4096]{1,0:T(8,128)S(1)} %copy-done.1, f32[4,16,4096]{2,1,0:T(8,128)S(1)} %copy-done, bf16[4,16,4096]{2,1,0:T(8,128)(2,1)S(1)} %copy-done.2, ...), custom_call_target="tpu_custom_call" | custom-call | tf_op jit(solution)/shard_map/prepare/pallas_call | solution.py:363
  8.1 0.0 collective-permute-done.modes_ref
  8.1 0.7 %more.2.binned_in = f32[32,4096]{1,0:T(8,128)S(1)} custom-call(f32[8,128]{1,0:T(8,128)S(1)} %get-tuple-element.22.refs_0_.efficiency_ref, f32[4,16,4096]{2,1,0:T(8,128)S(1)} %copy-done, bf16[128,4096]{1,0:T(8,128)(2,1)S(1)} %get-tuple-element.24.high_ref, bf16[128,4096]{1,0:T(8,128)(2,1)S(1)} %get-tuple-element.25.low_ref, ...), custom_call_target="tpu_custom_call" | custom-call | tf_op jit(solution)/shard_map/more/pallas_call | solution.py:374
  8.9 1.8 %collective-permute-done.1.modes_ref = f32[4,8,128]{2,1,0:T(8,128)S(1)} collective-permute-done((f32[4,8,128]{2,1,0:T(8,128)S(1)}, f32[4,8,128]{2,1,0:T(8,128)S(1)}, u32[]{:S(2)}, u32[]{:S(2)}) %collective-permute-start.1) | collective-permute-done | bytes 16416 | tf_op jit(solution)/shard_map/ppermute | solution.py:351
  10.7 0.7 %more.3.refs_0_ = f32[32,4096]{1,0:T(8,128)S(1)} custom-call(f32[8,128]{1,0:T(8,128)S(1)} %get-tuple-element.22.refs_0_.efficiency_ref, f32[4,16,4096]{2,1,0:T(8,128)S(1)} %copy-done, bf16[128,4096]{1,0:T(8,128)(2,1)S(1)} %get-tuple-element.24.high_ref, bf16[128,4096]{1,0:T(8,128)(2,1)S(1)} %get-tuple-element.25.low_ref, f32[32,4096]{1,0:T(8,128)S(1)} %more.2.binned_in, ...), custom_call_target="tpu_custom_call" | custom-call | tf_op jit(solution)/shard_map/more/pallas_call | solution.py:374
  11.4 0.0 collective-permute-done.2.refs_1_
  11.4 1.3 %maps.1 = f32[16,1,128]{2,1,0:T(1,128)S(1)} custom-call(f32[8,128]{1,0:T(8,128)S(1)} %get-tuple-element.22.refs_0_.efficiency_ref, f32[4,16,4096]{2,1,0:T(8,128)S(1)} %copy-done, bf16[128,4096]{1,0:T(8,128)(2,1)S(1)} %get-tuple-element.24.high_ref, bf16[128,4096]{1,0:T(8,128)(2,1)S(1)} %get-tuple-element.25.low_ref, ...), custom_call_target="tpu_custom_call" | custom-call | tf_op jit(solution)/shard_map/maps/pallas_call | solution.py:386
  12.7 9.9 %all_to_all.5.got_ref = f32[16,1,128]{2,1,0:T(1,128)S(1)} all-to-all(f32[16,1,128]{2,1,0:T(1,128)S(1)} %maps.1), channel_id=1, replica_groups=mesh['cosmo'=2,'shell'=4,'band'=4] {'shell','band'}, dimensions={0} | all-to-all | bytes 16384 | tf_op jit(solution)/shard_map/all_to_all | solution.py:400
  22.6 0.8 %unpack.1 = f32[12,2,16]{2,1,0:T(2,128)} custom-call(f32[16,1,128]{2,1,0:T(1,128)S(1)} %all_to_all.5.got_ref), custom_call_target="tpu_custom_call" | custom-call | tf_op jit(solution)/shard_map/unpack/pallas_call | solution.py:401
Async XLA Ops:
  0.9 5.9 %copy-start = (f32[4,16,4096]{2,1,0:T(8,128)S(1)}, f32[4,16,4096]{2,1,0:T(8,128)}, u32[]{:S(2)}) copy-start(f32[4,16,4096]{2,1,0:T(8,128)} %legendre_ref.7) | copy-start | bytes 3145732
  0.9 5.8 %copy-start.1 = (f32[128,4096]{1,0:T(8,128)S(1)}, f32[128,4096]{1,0:T(8,128)}, u32[]{:S(2)}) copy-start(f32[128,4096]{1,0:T(8,128)} %window_ref.1) | copy-start | bytes 6291460
  0.9 5.8 %copy-start.2 = (bf16[4,16,4096]{2,1,0:T(8,128)(2,1)S(1)}, bf16[4,16,4096]{2,1,0:T(8,128)(2,1)}, u32[]{:S(2)}) copy-start(bf16[4,16,4096]{2,1,0:T(8,128)(2,1)} %plus_ref.1) | copy-start | bytes 1572868
  0.9 5.8 %copy-start.3 = (bf16[4,16,4096]{2,1,0:T(8,128)(2,1)S(1)}, bf16[4,16,4096]{2,1,0:T(8,128)(2,1)}, u32[]{:S(2)}) copy-start(bf16[4,16,4096]{2,1,0:T(8,128)(2,1)} %minus_ref.1) | copy-start | bytes 1572868
  1.0 7.1 %collective-permute-start = (f32[4,8,128]{2,1,0:T(8,128)S(1)}, f32[4,8,128]{2,1,0:T(8,128)S(1)}, u32[]{:S(2)}, u32[]{:S(2)}) collective-permute-start(f32[4,8,128]{2,1,0:T(8,128)S(1)} %get-tuple-element.28), channel_id=1, source_target_pairs={{0,2},{1,3},{2,0},{3,1},{4,6},{5,7},{6,4},{7,5},{8,10},{9,11},{10,... | collective-permute-start | bytes 49160 | tf_op jit(solution)/shard_map/ppermute | solution.py:351
  5.2 5.5 %collective-permute-start.1 = (f32[4,8,128]{2,1,0:T(8,128)S(1)}, f32[4,8,128]{2,1,0:T(8,128)S(1)}, u32[]{:S(2)}, u32[]{:S(2)}) collective-permute-start(f32[4,8,128]{2,1,0:T(8,128)S(1)} %get-tuple-element.29), channel_id=1, source_target_pairs={{0,3},{1,2},{2,1},{3,0},{4,7},{5,6},{6,5},{7,4},{8,11},{9,10},{10,... | collective-permute-start | bytes 49160 | tf_op jit(solution)/shard_map/ppermute | solution.py:351
  6.5 4.9 %collective-permute-start.2 = (f32[4,8,128]{2,1,0:T(8,128)S(1)}, f32[4,8,128]{2,1,0:T(8,128)S(1)}, u32[]{:S(2)}, u32[]{:S(2)}) collective-permute-start(f32[4,8,128]{2,1,0:T(8,128)S(1)} %get-tuple-element.30), channel_id=1, source_target_pairs={{0,1},{1,0},{2,3},{3,2},{4,5},{5,4},{6,7},{7,6},{8,9},{9,8},{10,11... | collective-permute-start | bytes 49160 | tf_op jit(solution)/shard_map/ppermute | solution.py:351

commit v6 on v5

--- a/solution.py
+++ b/solution.py
@@ -10,6 +10,7 @@
 TILE = 256
 GROUP = 16
 LANES = 128
+ROUTES = ((0, 1, 2, 3), (2, 3, 1, 0), (1, 0, 3, 2), (3, 2, 0, 1))
 VMEM = pl.BlockSpec(memory_space=pltpu.VMEM)
 HBM = pl.BlockSpec(memory_space=pltpu.HBM)
 PARAMS = pltpu.CompilerParams(vmem_limit_bytes=28 * 2**20)
@@ -18,6 +19,15 @@
 
 def keep(x):
     return pltpu.with_memory_space_constraint(x, pltpu.HBM)
+
+
+def route(k, here, back=False):
+    bands = range(len(ROUTES[k]))
+    ends = tuple(ROUTES[k].index(z) for z in bands) if back else ROUTES[k]
+    end = jnp.int32(ends[0])
+    for z in bands[1:]:
+        end = jnp.where(here == z, ends[z], end)
+    return end
 
 
 def split(x):
@@ -52,7 +62,7 @@
     if offsets:
         here = lax.axis_index("band")
         for k, out_ref in zip((0, *offsets), out_refs):
-            out_ref[...] = blocks_ref[here ^ k]
+            out_ref[...] = blocks_ref[route(k, here)]
     else:
         out_refs[0][...] = blocks_ref[...]
     rows = 2 * bins
@@ -111,7 +121,7 @@
 def gather_left(modes_refs, efficiency_ref, left_ref, left_high_ref, orders, cycles_here, offsets):
     if offsets:
         here = lax.axis_index("band")
-        firsts = [((here ^ k) * cycles_here, cycles_here) for k in offsets]
+        firsts = [(route(k, here, True) * cycles_here, cycles_here) for k in offsets]
         modes = jnp.concatenate([ref[...] for ref in modes_refs], 0)
     else:
         modes = modes_refs[0][...]
@@ -306,7 +316,7 @@
     orders, cycles, degrees = legendre.shape
     bins = source_shell.shape[0]
     assert bins == shell_parts and 8 * orders * cycles_here == LANES
-    offsets = (2, 3, 1) if bands == 4 else ()
+    offsets = tuple(range(1, bands)) if bands == len(ROUTES) else ()
     rows = 2 * bins
     columns = 4 * orders * cycles
 
@@ -348,7 +358,7 @@
     if offsets:
         own, *sends = blocks
         got = [
-            lax.ppermute(send, "band", [(z, z ^ k) for z in range(bands)])
+            lax.ppermute(send, "band", [(z, ROUTES[k][z]) for z in range(bands)])
             for k, send in zip(offsets, sends)
         ]
     else:

time: 23.6 us -> 23.4 us (level)
  waiting for transfers between devices: 1.81 us -> 1.47 us
  starting transfers between devices: 5.71 us -> 6.03 us
    ppermute x3, waiting for transfers between devices: 1.81 us -> 1.47 us  [on_device(): lax.ppermute(send, 'band', [(z, ROUTES[k][z]) for z in range(bands)])]
    ppermute x3, starting transfers between devices: 5.71 us -> 6.03 us  [on_device(): lax.ppermute(send, 'band', [(z, ROUTES[k][z]) for z in range(bands)])]
where the time goes in v6:
time: 23.4 us; the launch traced here: 23.2 us
  blocking collectives  9.69 us (41%)
  starting transfers between devices  6.03 us (26%)
  Pallas kernels  5.88 us (25%)
  waiting for transfers between devices  1.47 us (6%)
    all_to_all x1, blocking collectives, on_device(): lax.all_to_all(maps, ('shell', 'band'), split_axis=0, concat_axis=0, tile...  9.69 us
    ppermute x3, starting transfers between devices, on_device(): lax.ppermute(send, 'band', [(z, ROUTES[k][z]) for z in range(bands)])  6.03 us
    ppermute x3, waiting for transfers between devices, on_device(): lax.ppermute(send, 'band', [(z, ROUTES[k][z]) for z in range(bands)])  1.47 us
    pallas_call x2, Pallas kernels, on_device(): pl.pallas_call(functools.partial(more_kernel, orders=orders, cycles_here=...  1.47 us
    pallas_call x1, Pallas kernels, on_device(): pl.pallas_call(functools.partial(prepare_kernel, orders=orders, cycles_he...  1.37 us
    pallas_call x1, Pallas kernels, on_device(): pl.pallas_call(functools.partial(maps_kernel, bands=bands, orders=orders,...  1.29 us
    pallas_call x1, Pallas kernels, on_device(): pl.pallas_call(load_kernel, in_specs=[HBM] * 4, out_specs=[VMEM] * 4, out...  0.88 us
    pallas_call x1, Pallas kernels, on_device(): pl.pallas_call(functools.partial(unpack_kernel, bands=bands, orders=order...  0.78 us
  transfers between devices with their start and end apart: 3, of which 1 were waited for; matrix products, arithmetic and copies ran while one was open for 0% of the time, Pallas kernels for 12%

profile of v6, /device:TPU:0, one launch (start us, length us, event | category | flops | bytes accessed | tf_op | source)
XLA Modules:
  0.0 23.2 jit_solution(2500411158078843763)
XLA Ops:
  0.0 0.9 %load.1 = (f32[4,2,16,128]{3,2,1,0:T(8,128)S(1)}, f32[1,4]{1,0:T(1,128)S(1)}, s32[1,4]{1,0:T(1,128)S(1)}, f32[1,128]{1,0:T(1,128)S(1)}) custom-call(f32[4,2,16,128]{3,2,1,0:T(8,128)} %bitcast.5, f32[1,4]{1,0:T(1,128)} %bitcast.6, s32[1,4]{1,0:T(1,128)} %bitcast.7, f32[1,128]{1,0:T(1,128)} %bitcast.8), custom_call_target="tpu_custom_call" | custom-call | tf_op jit(solution)/shard_map/load/pallas_call | solution.py:339
  0.9 0.0 copy-start
  0.9 0.0 copy-start.1
  0.9 0.0 copy-start.2
  0.9 0.0 copy-start.3
  0.9 0.1 pack.1
  1.0 4.1 %collective-permute-start = (f32[4,8,128]{2,1,0:T(8,128)S(1)}, f32[4,8,128]{2,1,0:T(8,128)S(1)}, u32[]{:S(2)}, u32[]{:S(2)}) collective-permute-start(f32[4,8,128]{2,1,0:T(8,128)S(1)} %get-tuple-element.28), channel_id=1, source_target_pairs={{0,2},{1,3},{2,1},{3,0},{4,6},{5,7},{6,5},{7,4},{8,10},{9,11},{10,... | collective-permute-start | bytes 49160 | tf_op jit(solution)/shard_map/ppermute | solution.py:361
  5.1 1.6 %collective-permute-start.1 = (f32[4,8,128]{2,1,0:T(8,128)S(1)}, f32[4,8,128]{2,1,0:T(8,128)S(1)}, u32[]{:S(2)}, u32[]{:S(2)}) collective-permute-start(f32[4,8,128]{2,1,0:T(8,128)S(1)} %get-tuple-element.29), channel_id=1, source_target_pairs={{0,1},{1,0},{2,3},{3,2},{4,5},{5,4},{6,7},{7,6},{8,9},{9,8},{10,11... | collective-permute-start | bytes 49160 | tf_op jit(solution)/shard_map/ppermute | solution.py:361
  6.7 0.3 %collective-permute-start.2 = (f32[4,8,128]{2,1,0:T(8,128)S(1)}, f32[4,8,128]{2,1,0:T(8,128)S(1)}, u32[]{:S(2)}, u32[]{:S(2)}) collective-permute-start(f32[4,8,128]{2,1,0:T(8,128)S(1)} %get-tuple-element.30), channel_id=1, source_target_pairs={{0,3},{1,2},{2,0},{3,1},{4,7},{5,6},{6,4},{7,5},{8,11},{9,10},{10,... | collective-permute-start | bytes 49160 | tf_op jit(solution)/shard_map/ppermute | solution.py:361
  7.1 0.0 copy-done
  7.1 0.0 copy-done.1
  7.1 0.0 copy-done.2
  7.1 0.0 copy-done.3
  7.1 1.4 %prepare.1 = (bf16[128,4096]{1,0:T(8,128)(2,1)S(1)}, bf16[128,4096]{1,0:T(8,128)(2,1)S(1)}, bf16[4096,256]{1,0:T(8,128)(2,1)S(1)}, f32[32,4096]{1,0:T(8,128)S(1)}) custom-call(f32[128,4096]{1,0:T(8,128)S(1)} %copy-done.1, f32[4,16,4096]{2,1,0:T(8,128)S(1)} %copy-done, bf16[4,16,4096]{2,1,0:T(8,128)(2,1)S(1)} %copy-done.2, ...), custom_call_target="tpu_custom_call" | custom-call | tf_op jit(solution)/shard_map/prepare/pallas_call | solution.py:373
  8.5 0.0 collective-permute-done.modes_ref
  8.5 0.7 %more.2.binned_in = f32[32,4096]{1,0:T(8,128)S(1)} custom-call(f32[8,128]{1,0:T(8,128)S(1)} %get-tuple-element.22.refs_0_.efficiency_ref, f32[4,16,4096]{2,1,0:T(8,128)S(1)} %copy-done, bf16[128,4096]{1,0:T(8,128)(2,1)S(1)} %get-tuple-element.24.high_ref, bf16[128,4096]{1,0:T(8,128)(2,1)S(1)} %get-tuple-element.25.low_ref, ...), custom_call_target="tpu_custom_call" | custom-call | tf_op jit(solution)/shard_map/more/pallas_call | solution.py:384
  9.2 0.0 collective-permute-done.1.modes_ref
  9.2 0.7 %more.3.refs_0_ = f32[32,4096]{1,0:T(8,128)S(1)} custom-call(f32[8,128]{1,0:T(8,128)S(1)} %get-tuple-element.22.refs_0_.efficiency_ref, f32[4,16,4096]{2,1,0:T(8,128)S(1)} %copy-done, bf16[128,4096]{1,0:T(8,128)(2,1)S(1)} %get-tuple-element.24.high_ref, bf16[128,4096]{1,0:T(8,128)(2,1)S(1)} %get-tuple-element.25.low_ref, f32[32,4096]{1,0:T(8,128)S(1)} %more.2.binned_in, ...), custom_call_target="tpu_custom_call" | custom-call | tf_op jit(solution)/shard_map/more/pallas_call | solution.py:384
  10.0 1.5 %collective-permute-done.2.refs_1_ = f32[4,8,128]{2,1,0:T(8,128)S(1)} collective-permute-done((f32[4,8,128]{2,1,0:T(8,128)S(1)}, f32[4,8,128]{2,1,0:T(8,128)S(1)}, u32[]{:S(2)}, u32[]{:S(2)}) %collective-permute-start.2) | collective-permute-done | bytes 16416 | tf_op jit(solution)/shard_map/ppermute | solution.py:361
  11.4 1.3 %maps.1 = f32[16,1,128]{2,1,0:T(1,128)S(1)} custom-call(f32[8,128]{1,0:T(8,128)S(1)} %get-tuple-element.22.refs_0_.efficiency_ref, f32[4,16,4096]{2,1,0:T(8,128)S(1)} %copy-done, bf16[128,4096]{1,0:T(8,128)(2,1)S(1)} %get-tuple-element.24.high_ref, bf16[128,4096]{1,0:T(8,128)(2,1)S(1)} %get-tuple-element.25.low_ref, ...), custom_call_target="tpu_custom_call" | custom-call | tf_op jit(solution)/shard_map/maps/pallas_call | solution.py:396
  12.7 9.7 %all_to_all.5.got_ref = f32[16,1,128]{2,1,0:T(1,128)S(1)} all-to-all(f32[16,1,128]{2,1,0:T(1,128)S(1)} %maps.1), channel_id=1, replica_groups=mesh['cosmo'=2,'shell'=4,'band'=4] {'shell','band'}, dimensions={0} | all-to-all | bytes 16384 | tf_op jit(solution)/shard_map/all_to_all | solution.py:410
  22.4 0.8 %unpack.1 = f32[12,2,16]{2,1,0:T(2,128)} custom-call(f32[16,1,128]{2,1,0:T(1,128)S(1)} %all_to_all.5.got_ref), custom_call_target="tpu_custom_call" | custom-call | tf_op jit(solution)/shard_map/unpack/pallas_call | solution.py:411
Async XLA Ops:
  0.9 6.2 %copy-start = (f32[4,16,4096]{2,1,0:T(8,128)S(1)}, f32[4,16,4096]{2,1,0:T(8,128)}, u32[]{:S(2)}) copy-start(f32[4,16,4096]{2,1,0:T(8,128)} %legendre_ref.7) | copy-start | bytes 3145732
  0.9 6.2 %copy-start.1 = (f32[128,4096]{1,0:T(8,128)S(1)}, f32[128,4096]{1,0:T(8,128)}, u32[]{:S(2)}) copy-start(f32[128,4096]{1,0:T(8,128)} %window_ref.1) | copy-start | bytes 6291460
  0.9 6.2 %copy-start.2 = (bf16[4,16,4096]{2,1,0:T(8,128)(2,1)S(1)}, bf16[4,16,4096]{2,1,0:T(8,128)(2,1)}, u32[]{:S(2)}) copy-start(bf16[4,16,4096]{2,1,0:T(8,128)(2,1)} %plus_ref.1) | copy-start | bytes 1572868
  0.9 6.1 %copy-start.3 = (bf16[4,16,4096]{2,1,0:T(8,128)(2,1)S(1)}, bf16[4,16,4096]{2,1,0:T(8,128)(2,1)}, u32[]{:S(2)}) copy-start(bf16[4,16,4096]{2,1,0:T(8,128)(2,1)} %minus_ref.1) | copy-start | bytes 1572868
  1.0 7.4 %collective-permute-start = (f32[4,8,128]{2,1,0:T(8,128)S(1)}, f32[4,8,128]{2,1,0:T(8,128)S(1)}, u32[]{:S(2)}, u32[]{:S(2)}) collective-permute-start(f32[4,8,128]{2,1,0:T(8,128)S(1)} %get-tuple-element.28), channel_id=1, source_target_pairs={{0,2},{1,3},{2,1},{3,0},{4,6},{5,7},{6,5},{7,4},{8,10},{9,11},{10,... | collective-permute-start | bytes 49160 | tf_op jit(solution)/shard_map/ppermute | solution.py:361
  5.1 4.1 %collective-permute-start.1 = (f32[4,8,128]{2,1,0:T(8,128)S(1)}, f32[4,8,128]{2,1,0:T(8,128)S(1)}, u32[]{:S(2)}, u32[]{:S(2)}) collective-permute-start(f32[4,8,128]{2,1,0:T(8,128)S(1)} %get-tuple-element.29), channel_id=1, source_target_pairs={{0,1},{1,0},{2,3},{3,2},{4,5},{5,4},{6,7},{7,6},{8,9},{9,8},{10,11... | collective-permute-start | bytes 49160 | tf_op jit(solution)/shard_map/ppermute | solution.py:361
  6.7 4.7 %collective-permute-start.2 = (f32[4,8,128]{2,1,0:T(8,128)S(1)}, f32[4,8,128]{2,1,0:T(8,128)S(1)}, u32[]{:S(2)}, u32[]{:S(2)}) collective-permute-start(f32[4,8,128]{2,1,0:T(8,128)S(1)} %get-tuple-element.30), channel_id=1, source_target_pairs={{0,3},{1,2},{2,0},{3,1},{4,7},{5,6},{6,4},{7,5},{8,11},{9,10},{10,... | collective-permute-start | bytes 49160 | tf_op jit(solution)/shard_map/ppermute | solution.py:361

commit v7 on v6

--- a/solution.py
+++ b/solution.py
@@ -229,11 +229,9 @@
             multiply(left_ref[...], left_high_ref[...], high_ref[:, lanes], low_ref[:, lanes]) for lanes in spans
         ]
         lefts = [coefficients(*pair) for pair in zip(starts, products)]
-        parts = [
-            jnp.dot(left, tables_ref[lanes, :], preferred_element_type=jnp.float32)
-            for left, lanes in zip(lefts, spans)
-        ]
-        sums_ref[...] += sum(parts[1:], parts[0])
+        sums_ref[...] += jnp.dot(
+            jnp.concatenate(lefts, 1), tables_ref[pl.ds(start, group * TILE), :], preferred_element_type=jnp.float32
+        )
 
     each_tile(legendre_ref.shape[2], bool(offsets), step, group * TILE)
 
@@ -299,9 +297,13 @@
         jnp.where(table <= KAPPA_LOW, same, 0.0),
         jnp.where(field == 1, jnp.where(table == PLUS, same, 0.0), jnp.where(table == MINUS, other, 0.0)),
     )
+    values = jnp.concatenate(values, 0)
+    high, _ = split(values)
+    middle, low = split(values - high.astype(jnp.float32))
+    pick = jnp.where(lane % cycles_here == cycle, pick, 0.0).astype(jnp.bfloat16)
     maps = lax.dot_general(
-        jnp.where(lane % cycles_here == cycle, pick, 0.0), jnp.concatenate(values, 0), (((1,), (1,)), ((), ())),
-        precision=lax.Precision.HIGHEST, preferred_element_type=jnp.float32,
+        jnp.concatenate([pick] * 3, 1), jnp.concatenate([high, middle, low], 1), (((1,), (1,)), ((), ())),
+        preferred_element_type=jnp.float32,
     )
     for i in range(3 * cycles_here):
         out_ref[i] = maps[2 * i : 2 * i + 2]

time: 23.4 us -> 23.3 us (level)
  no operation moved by 1% of the time
where the time goes in v7:
time: 23.3 us; the launch traced here: 23.1 us
  blocking collectives  9.68 us (42%)
  starting transfers between devices  6.03 us (26%)
  Pallas kernels  5.83 us (25%)
  waiting for transfers between devices  1.47 us (6%)
    all_to_all x1, blocking collectives, on_device(): lax.all_to_all(maps, ('shell', 'band'), split_axis=0, concat_axis=0, tile...  9.68 us
    ppermute x3, starting transfers between devices, on_device(): lax.ppermute(send, 'band', [(z, ROUTES[k][z]) for z in range(bands)])  6.03 us
    ppermute x3, waiting for transfers between devices, on_device(): lax.ppermute(send, 'band', [(z, ROUTES[k][z]) for z in range(bands)])  1.47 us
    pallas_call x2, Pallas kernels, on_device(): pl.pallas_call(functools.partial(more_kernel, orders=orders, cycles_here=...  1.47 us
    pallas_call x1, Pallas kernels, on_device(): pl.pallas_call(functools.partial(prepare_kernel, orders=orders, cycles_he...  1.37 us
    pallas_call x1, Pallas kernels, on_device(): pl.pallas_call(functools.partial(maps_kernel, bands=bands, orders=orders,...  1.26 us
    pallas_call x1, Pallas kernels, on_device(): pl.pallas_call(load_kernel, in_specs=[HBM] * 4, out_specs=[VMEM] * 4, out...  0.88 us
    pallas_call x1, Pallas kernels, on_device(): pl.pallas_call(functools.partial(unpack_kernel, bands=bands, orders=order...  0.76 us
  transfers between devices with their start and end apart: 3, of which 1 were waited for; matrix products, arithmetic and copies ran while one was open for 0% of the time, Pallas kernels for 12%

profile of v7, /device:TPU:0, one launch (start us, length us, event | category | flops | bytes accessed | tf_op | source)
XLA Modules:
  0.0 23.1 jit_solution(14675478545754167614)
XLA Ops:
  0.0 0.9 %load.1 = (f32[4,2,16,128]{3,2,1,0:T(8,128)S(1)}, f32[1,4]{1,0:T(1,128)S(1)}, s32[1,4]{1,0:T(1,128)S(1)}, f32[1,128]{1,0:T(1,128)S(1)}) custom-call(f32[4,2,16,128]{3,2,1,0:T(8,128)} %bitcast.5, f32[1,4]{1,0:T(1,128)} %bitcast.6, s32[1,4]{1,0:T(1,128)} %bitcast.7, f32[1,128]{1,0:T(1,128)} %bitcast.8), custom_call_target="tpu_custom_call" | custom-call | tf_op jit(solution)/shard_map/load/pallas_call | solution.py:341
  0.9 0.0 copy-start
  0.9 0.0 copy-start.1
  0.9 0.0 copy-start.2
  0.9 0.0 copy-start.3
  0.9 0.1 pack.1
  1.0 4.1 %collective-permute-start = (f32[4,8,128]{2,1,0:T(8,128)S(1)}, f32[4,8,128]{2,1,0:T(8,128)S(1)}, u32[]{:S(2)}, u32[]{:S(2)}) collective-permute-start(f32[4,8,128]{2,1,0:T(8,128)S(1)} %get-tuple-element.28), channel_id=1, source_target_pairs={{0,2},{1,3},{2,1},{3,0},{4,6},{5,7},{6,5},{7,4},{8,10},{9,11},{10,... | collective-permute-start | bytes 49160 | tf_op jit(solution)/shard_map/ppermute | solution.py:363
  5.1 1.6 %collective-permute-start.1 = (f32[4,8,128]{2,1,0:T(8,128)S(1)}, f32[4,8,128]{2,1,0:T(8,128)S(1)}, u32[]{:S(2)}, u32[]{:S(2)}) collective-permute-start(f32[4,8,128]{2,1,0:T(8,128)S(1)} %get-tuple-element.29), channel_id=1, source_target_pairs={{0,1},{1,0},{2,3},{3,2},{4,5},{5,4},{6,7},{7,6},{8,9},{9,8},{10,11... | collective-permute-start | bytes 49160 | tf_op jit(solution)/shard_map/ppermute | solution.py:363
  6.7 0.3 %collective-permute-start.2 = (f32[4,8,128]{2,1,0:T(8,128)S(1)}, f32[4,8,128]{2,1,0:T(8,128)S(1)}, u32[]{:S(2)}, u32[]{:S(2)}) collective-permute-start(f32[4,8,128]{2,1,0:T(8,128)S(1)} %get-tuple-element.30), channel_id=1, source_target_pairs={{0,3},{1,2},{2,0},{3,1},{4,7},{5,6},{6,4},{7,5},{8,11},{9,10},{10,... | collective-permute-start | bytes 49160 | tf_op jit(solution)/shard_map/ppermute | solution.py:363
  7.1 0.0 copy-done
  7.1 0.0 copy-done.1
  7.1 0.0 copy-done.2
  7.1 0.0 copy-done.3
  7.1 1.4 %prepare.1 = (bf16[128,4096]{1,0:T(8,128)(2,1)S(1)}, bf16[128,4096]{1,0:T(8,128)(2,1)S(1)}, bf16[4096,256]{1,0:T(8,128)(2,1)S(1)}, f32[32,4096]{1,0:T(8,128)S(1)}) custom-call(f32[128,4096]{1,0:T(8,128)S(1)} %copy-done.1, f32[4,16,4096]{2,1,0:T(8,128)S(1)} %copy-done, bf16[4,16,4096]{2,1,0:T(8,128)(2,1)S(1)} %copy-done.2, ...), custom_call_target="tpu_custom_call" | custom-call | tf_op jit(solution)/shard_map/prepare/pallas_call | solution.py:375
  8.5 0.0 collective-permute-done.modes_ref
  8.5 0.7 %more.2.binned_in = f32[32,4096]{1,0:T(8,128)S(1)} custom-call(f32[8,128]{1,0:T(8,128)S(1)} %get-tuple-element.22.refs_0_.efficiency_ref, f32[4,16,4096]{2,1,0:T(8,128)S(1)} %copy-done, bf16[128,4096]{1,0:T(8,128)(2,1)S(1)} %get-tuple-element.24.high_ref, bf16[128,4096]{1,0:T(8,128)(2,1)S(1)} %get-tuple-element.25.low_ref, ...), custom_call_target="tpu_custom_call" | custom-call | tf_op jit(solution)/shard_map/more/pallas_call | solution.py:386
  9.2 0.0 collective-permute-done.1.modes_ref
  9.2 0.7 %more.3.refs_0_ = f32[32,4096]{1,0:T(8,128)S(1)} custom-call(f32[8,128]{1,0:T(8,128)S(1)} %get-tuple-element.22.refs_0_.efficiency_ref, f32[4,16,4096]{2,1,0:T(8,128)S(1)} %copy-done, bf16[128,4096]{1,0:T(8,128)(2,1)S(1)} %get-tuple-element.24.high_ref, bf16[128,4096]{1,0:T(8,128)(2,1)S(1)} %get-tuple-element.25.low_ref, f32[32,4096]{1,0:T(8,128)S(1)} %more.2.binned_in, ...), custom_call_target="tpu_custom_call" | custom-call | tf_op jit(solution)/shard_map/more/pallas_call | solution.py:386
  10.0 1.5 %collective-permute-done.2.refs_1_ = f32[4,8,128]{2,1,0:T(8,128)S(1)} collective-permute-done((f32[4,8,128]{2,1,0:T(8,128)S(1)}, f32[4,8,128]{2,1,0:T(8,128)S(1)}, u32[]{:S(2)}, u32[]{:S(2)}) %collective-permute-start.2) | collective-permute-done | bytes 16416 | tf_op jit(solution)/shard_map/ppermute | solution.py:363
  11.4 1.3 %maps.1 = f32[16,1,128]{2,1,0:T(1,128)S(1)} custom-call(f32[8,128]{1,0:T(8,128)S(1)} %get-tuple-element.22.refs_0_.efficiency_ref, f32[4,16,4096]{2,1,0:T(8,128)S(1)} %copy-done, bf16[128,4096]{1,0:T(8,128)(2,1)S(1)} %get-tuple-element.24.high_ref, bf16[128,4096]{1,0:T(8,128)(2,1)S(1)} %get-tuple-element.25.low_ref, ...), custom_call_target="tpu_custom_call" | custom-call | tf_op jit(solution)/shard_map/maps/pallas_call | solution.py:398
  12.7 9.7 %all_to_all.5.got_ref = f32[16,1,128]{2,1,0:T(1,128)S(1)} all-to-all(f32[16,1,128]{2,1,0:T(1,128)S(1)} %maps.1), channel_id=1, replica_groups=mesh['cosmo'=2,'shell'=4,'band'=4] {'shell','band'}, dimensions={0} | all-to-all | bytes 16384 | tf_op jit(solution)/shard_map/all_to_all | solution.py:412
  22.4 0.8 %unpack.1 = f32[12,2,16]{2,1,0:T(2,128)} custom-call(f32[16,1,128]{2,1,0:T(1,128)S(1)} %all_to_all.5.got_ref), custom_call_target="tpu_custom_call" | custom-call | tf_op jit(solution)/shard_map/unpack/pallas_call | solution.py:413
Async XLA Ops:
  0.9 6.2 %copy-start = (f32[4,16,4096]{2,1,0:T(8,128)S(1)}, f32[4,16,4096]{2,1,0:T(8,128)}, u32[]{:S(2)}) copy-start(f32[4,16,4096]{2,1,0:T(8,128)} %legendre_ref.7) | copy-start | bytes 3145732
  0.9 6.2 %copy-start.1 = (f32[128,4096]{1,0:T(8,128)S(1)}, f32[128,4096]{1,0:T(8,128)}, u32[]{:S(2)}) copy-start(f32[128,4096]{1,0:T(8,128)} %window_ref.1) | copy-start | bytes 6291460
  0.9 6.2 %copy-start.2 = (bf16[4,16,4096]{2,1,0:T(8,128)(2,1)S(1)}, bf16[4,16,4096]{2,1,0:T(8,128)(2,1)}, u32[]{:S(2)}) copy-start(bf16[4,16,4096]{2,1,0:T(8,128)(2,1)} %plus_ref.1) | copy-start | bytes 1572868
  0.9 6.1 %copy-start.3 = (bf16[4,16,4096]{2,1,0:T(8,128)(2,1)S(1)}, bf16[4,16,4096]{2,1,0:T(8,128)(2,1)}, u32[]{:S(2)}) copy-start(bf16[4,16,4096]{2,1,0:T(8,128)(2,1)} %minus_ref.1) | copy-start | bytes 1572868
  1.0 7.4 %collective-permute-start = (f32[4,8,128]{2,1,0:T(8,128)S(1)}, f32[4,8,128]{2,1,0:T(8,128)S(1)}, u32[]{:S(2)}, u32[]{:S(2)}) collective-permute-start(f32[4,8,128]{2,1,0:T(8,128)S(1)} %get-tuple-element.28), channel_id=1, source_target_pairs={{0,2},{1,3},{2,1},{3,0},{4,6},{5,7},{6,5},{7,4},{8,10},{9,11},{10,... | collective-permute-start | bytes 49160 | tf_op jit(solution)/shard_map/ppermute | solution.py:363
  5.1 4.1 %collective-permute-start.1 = (f32[4,8,128]{2,1,0:T(8,128)S(1)}, f32[4,8,128]{2,1,0:T(8,128)S(1)}, u32[]{:S(2)}, u32[]{:S(2)}) collective-permute-start(f32[4,8,128]{2,1,0:T(8,128)S(1)} %get-tuple-element.29), channel_id=1, source_target_pairs={{0,1},{1,0},{2,3},{3,2},{4,5},{5,4},{6,7},{7,6},{8,9},{9,8},{10,11... | collective-permute-start | bytes 49160 | tf_op jit(solution)/shard_map/ppermute | solution.py:363
  6.7 4.7 %collective-permute-start.2 = (f32[4,8,128]{2,1,0:T(8,128)S(1)}, f32[4,8,128]{2,1,0:T(8,128)S(1)}, u32[]{:S(2)}, u32[]{:S(2)}) collective-permute-start(f32[4,8,128]{2,1,0:T(8,128)S(1)} %get-tuple-element.30), channel_id=1, source_target_pairs={{0,3},{1,2},{2,0},{3,1},{4,7},{5,6},{6,4},{7,5},{8,11},{9,10},{10,... | collective-permute-start | bytes 49160 | tf_op jit(solution)/shard_map/ppermute | solution.py:363

commit v8 on v6

--- a/solution.py
+++ b/solution.py
@@ -22,10 +22,9 @@
 
 
 def route(k, here, back=False):
-    bands = range(len(ROUTES[k]))
-    ends = tuple(ROUTES[k].index(z) for z in bands) if back else ROUTES[k]
+    ends = tuple(ROUTES[k].index(z) for z in range(4)) if back else ROUTES[k]
     end = jnp.int32(ends[0])
-    for z in bands[1:]:
+    for z in range(1, 4):
         end = jnp.where(here == z, ends[z], end)
     return end
 
@@ -49,8 +48,8 @@
         copy.wait()
 
 
-def pack_kernel(modes_ref, weight_ref, source_ref, lensing_ref, *refs, bands, orders, bins, offsets):
-    *out_refs, efficiency_ref, blocks_ref = refs
+def pack_kernel(modes_ref, weight_ref, *refs, bands, orders, offsets):
+    *out_refs, blocks_ref = refs
     cycles_here, _, _, shells = modes_ref.shape
     for r in range(cycles_here):
         weight = jnp.broadcast_to(weight_ref[0:1, r : r + 1], (orders, shells))
@@ -65,13 +64,17 @@
             out_ref[...] = blocks_ref[route(k, here)]
     else:
         out_refs[0][...] = blocks_ref[...]
+
+
+def efficiency_of(source_ref, lensing_ref, bins):
+    shells = lensing_ref.shape[1]
     rows = 2 * bins
     row_bin = iota((rows, shells), 0) % bins
     source = jnp.zeros((rows, shells), jnp.int32)
     for b in range(bins):
         source = jnp.where(row_bin == b, jnp.broadcast_to(source_ref[0:1, b : b + 1], (rows, shells)), source)
     shell_ids = lax.axis_index("shell") * shells + iota((rows, shells), 1)
-    efficiency_ref[...] = (
+    return (
         lensing_ref[...]
         * jnp.maximum(source - shell_ids, 0).astype(jnp.float32)
         / (source + 1).astype(jnp.float32)
@@ -133,15 +136,17 @@
     return firsts
 
 
-def prepare_kernel(window_ref, legendre_ref, plus_ref, minus_ref, *refs, orders, cycles_here):
-    if len(refs) > 3:
-        efficiency_ref, own_ref, *refs, binned_ref, left_ref, left_high_ref = refs
-        rows = efficiency_ref.shape[0]
+def prepare_kernel(
+    source_ref, lensing_ref, window_ref, legendre_ref, plus_ref, minus_ref, *refs, orders, cycles_here,
+):
+    own = len(refs) > 4
+    if own:
+        own_ref, *refs, binned_ref, left_ref, left_high_ref = refs
+    efficiency_ref, high_ref, low_ref, tables_ref = refs
+    rows = efficiency_ref.shape[0]
+    efficiency_ref[...] = efficiency_of(source_ref, lensing_ref, rows // 2)
+    if own:
         firsts = gather_left([own_ref], efficiency_ref, left_ref, left_high_ref, orders, cycles_here, (0,))
-        own = True
-    else:
-        own = False
-    high_ref, low_ref, tables_ref = refs
     columns = legendre_ref.shape[0] * legendre_ref.shape[1]
     same = jnp.where(iota((TILE, TILE), 0) == iota((TILE, TILE), 1), 1.0, 0.0).astype(jnp.bfloat16)
 
@@ -169,11 +174,11 @@
 
 
 def more_kernel(
-    efficiency_ref, legendre_ref, high_ref, low_ref, binned_in, modes_ref, binned_ref, left_ref, left_high_ref,
-    *, orders, cycles_here, offset,
+    efficiency_ref, legendre_ref, high_ref, low_ref, binned_in, *refs, orders, cycles_here, offsets,
 ):
+    *modes_refs, binned_ref, left_ref, left_high_ref = refs
     rows = efficiency_ref.shape[0]
-    firsts = gather_left([modes_ref], efficiency_ref, left_ref, left_high_ref, orders, cycles_here, (offset,))
+    firsts = gather_left(modes_refs, efficiency_ref, left_ref, left_high_ref, orders, cycles_here, offsets)
 
     def step(start):
         lanes = pl.ds(start, TILE)
@@ -316,7 +321,7 @@
     orders, cycles, degrees = legendre.shape
     bins = source_shell.shape[0]
     assert bins == shell_parts and 8 * orders * cycles_here == LANES
-    offsets = tuple(range(1, bands)) if bands == len(ROUTES) else ()
+    offsets = (1, 2, 3) if bands == 4 else ()
     rows = 2 * bins
     columns = 4 * orders * cycles
 
@@ -331,23 +336,19 @@
 
     block_shape = (cycles_here, 2 * orders, shells)
     out_shape = [shaped(*block_shape)] * bands if offsets else [shaped(bands, *block_shape)]
-    out_shape = [*out_shape, shaped(rows, shells)]
-    sources = (
-        cycle_modes.transpose(1, 2, 3, 0), cycle_weight.reshape(1, cycles_here),
-        source_shell.reshape(1, bins), lensing.reshape(1, shells),
-    )
+    sources = cycle_modes.transpose(1, 2, 3, 0), cycle_weight.reshape(1, cycles_here)
     sources = pl.pallas_call(
         load_kernel,
-        in_specs=[HBM] * 4,
-        out_specs=[VMEM] * 4,
-        out_shape=[shaped(*x.shape, dtype=x.dtype) for x in sources],
-        scratch_shapes=[pltpu.SemaphoreType.DMA((4,))],
+        in_specs=[HBM] * 2,
+        out_specs=[VMEM] * 2,
+        out_shape=[shaped(*x.shape) for x in sources],
+        scratch_shapes=[pltpu.SemaphoreType.DMA((2,))],
         compiler_params=PARAMS,
         name="load",
     )(*map(keep, sources))
-    *blocks, efficiency = pl.pallas_call(
-        functools.partial(pack_kernel, bands=bands, orders=orders, bins=bins, offsets=offsets),
-        in_specs=[VMEM] * 4,
+    blocks = pl.pallas_call(
+        functools.partial(pack_kernel, bands=bands, orders=orders, offsets=offsets),
+        in_specs=[VMEM] * 2,
         out_specs=[VMEM] * len(out_shape),
         out_shape=out_shape,
         scratch_shapes=[pltpu.VMEM((bands, *block_shape), jnp.float32)],
@@ -364,13 +365,15 @@
     else:
         got = [lax.all_to_all(blocks[0], "band", split_axis=0, concat_axis=0, tiled=True)]
     half = jnp.bfloat16
-    tables = [shaped(shells, degrees, dtype=half)] * 2 + [shaped(degrees, columns, dtype=half)]
+    tables = [shaped(rows, shells)] + [shaped(shells, degrees, dtype=half)] * 2 + [shaped(degrees, columns, dtype=half)]
     binned_shape = shaped(orders * rows, degrees)
-    arguments = [window, legendre, spin_plus, spin_minus]
+    arguments = [
+        source_shell.reshape(1, bins), lensing.reshape(1, shells), window, legendre, spin_plus, spin_minus,
+    ]
     if offsets:
         tables.append(binned_shape)
-        arguments += [efficiency, own]
-    high, low, turned, *binned = pl.pallas_call(
+        arguments.append(own)
+    efficiency, high, low, turned, *binned = pl.pallas_call(
         functools.partial(prepare_kernel, orders=orders, cycles_here=cycles_here),
         in_specs=[VMEM] * len(arguments),
         out_specs=[VMEM] * len(tables),
@@ -379,17 +382,18 @@
         compiler_params=PARAMS,
         name="prepare",
     )(*arguments)
-    for k, block in zip(offsets[:-1], got):
+    if offsets:
+        early = got[:-1]
         binned = [
             pl.pallas_call(
-                functools.partial(more_kernel, orders=orders, cycles_here=cycles_here, offset=k),
-                in_specs=[VMEM] * 6,
+                functools.partial(more_kernel, orders=orders, cycles_here=cycles_here, offsets=offsets[:-1]),
+                in_specs=[VMEM] * (5 + len(early)),
                 out_specs=VMEM,
                 out_shape=binned_shape,
-                scratch_shapes=left_scratch(1),
+                scratch_shapes=left_scratch(len(early)),
                 compiler_params=PARAMS,
                 name="more",
-            )(efficiency, legendre, high, low, *binned, block)
+            )(efficiency, legendre, high, low, *binned, *early)
         ]
     last = got[-1:]
     operands = [efficiency, legendre, high, low, turned, *binned, *last]

time: 23.4 us -> 23.3 us (level)
    pallas_call x2 -> x1, Pallas kernels: 1.47 us -> 1.27 us  [on_device(): pl.pallas_call(functools.partial(more_kernel, orders=orders, cycles_here=...]
  transfers between devices with their start and end apart: 3 -> 3, of which waited for: 1 -> 2; matrix products, arithmetic and copies ran while one was open for 0% -> 0% of each run, Pallas kernels for 12% -> 12%
where the time goes in v8:
time: 23.3 us; the launch traced here: 23.1 us
  blocking collectives  9.68 us (42%)
  starting transfers between devices  6.03 us (26%)
  Pallas kernels  5.72 us (25%)
  waiting for transfers between devices  1.55 us (7%)
    all_to_all x1, blocking collectives, on_device(): lax.all_to_all(maps, ('shell', 'band'), split_axis=0, concat_axis=0, tile...  9.68 us
    ppermute x3, starting transfers between devices, on_device(): lax.ppermute(send, 'band', [(z, ROUTES[k][z]) for z in range(bands)])  6.03 us
    ppermute x3, waiting for transfers between devices, on_device(): lax.ppermute(send, 'band', [(z, ROUTES[k][z]) for z in range(bands)])  1.55 us
    pallas_call x1, Pallas kernels, on_device(): pl.pallas_call(functools.partial(prepare_kernel, orders=orders, cycles_he...  1.49 us
    pallas_call x1, Pallas kernels, on_device(): pl.pallas_call(functools.partial(more_kernel, orders=orders, cycles_here=...  1.27 us
    pallas_call x1, Pallas kernels, on_device(): pl.pallas_call(functools.partial(maps_kernel, bands=bands, orders=orders,...  1.24 us
    pallas_call x1, Pallas kernels, on_device(): pl.pallas_call(load_kernel, in_specs=[HBM] * 2, out_specs=[VMEM] * 2, out...  0.86 us
    pallas_call x1, Pallas kernels, on_device(): pl.pallas_call(functools.partial(unpack_kernel, bands=bands, orders=order...  0.78 us
  transfers between devices with their start and end apart: 3, of which 2 were waited for; matrix products, arithmetic and copies ran while one was open for 0% of the time, Pallas kernels for 12%

profile of v8, /device:TPU:0, one launch (start us, length us, event | category | flops | bytes accessed | tf_op | source)
XLA Modules:
  0.0 23.1 jit_solution(12895872183570843520)
XLA Ops:
  0.0 0.9 %load.1 = (f32[4,2,16,128]{3,2,1,0:T(8,128)S(1)}, f32[1,4]{1,0:T(1,128)S(1)}) custom-call(f32[4,2,16,128]{3,2,1,0:T(8,128)} %bitcast.7, f32[1,4]{1,0:T(1,128)} %bitcast.8), custom_call_target="tpu_custom_call" | custom-call | tf_op jit(solution)/shard_map/load/pallas_call | solution.py:340
  0.9 0.0 copy-start
  0.9 0.0 copy-start.1
  0.9 0.0 copy-start.2
  0.9 0.0 copy-start.3
  0.9 0.0 copy-start.4
  0.9 0.0 copy-start.5
  0.9 0.1 pack.1
  1.0 4.1 %collective-permute-start = (f32[4,8,128]{2,1,0:T(8,128)S(1)}, f32[4,8,128]{2,1,0:T(8,128)S(1)}, u32[]{:S(2)}, u32[]{:S(2)}) collective-permute-start(f32[4,8,128]{2,1,0:T(8,128)S(1)} %get-tuple-element.24), channel_id=1, source_target_pairs={{0,2},{1,3},{2,1},{3,0},{4,6},{5,7},{6,5},{7,4},{8,10},{9,11},{10,... | collective-permute-start | bytes 49160 | tf_op jit(solution)/shard_map/ppermute | solution.py:362
  5.1 1.6 %collective-permute-start.1 = (f32[4,8,128]{2,1,0:T(8,128)S(1)}, f32[4,8,128]{2,1,0:T(8,128)S(1)}, u32[]{:S(2)}, u32[]{:S(2)}) collective-permute-start(f32[4,8,128]{2,1,0:T(8,128)S(1)} %get-tuple-element.25), channel_id=1, source_target_pairs={{0,1},{1,0},{2,3},{3,2},{4,5},{5,4},{6,7},{7,6},{8,9},{9,8},{10,11... | collective-permute-start | bytes 49160 | tf_op jit(solution)/shard_map/ppermute | solution.py:362
  6.7 0.3 %collective-permute-start.2 = (f32[4,8,128]{2,1,0:T(8,128)S(1)}, f32[4,8,128]{2,1,0:T(8,128)S(1)}, u32[]{:S(2)}, u32[]{:S(2)}) collective-permute-start(f32[4,8,128]{2,1,0:T(8,128)S(1)} %get-tuple-element.26), channel_id=1, source_target_pairs={{0,3},{1,2},{2,0},{3,1},{4,7},{5,6},{6,4},{7,5},{8,11},{9,10},{10,... | collective-permute-start | bytes 49160 | tf_op jit(solution)/shard_map/ppermute | solution.py:362
  7.1 0.0 copy-done
  7.1 0.0 copy-done.1
  7.1 0.0 copy-done.2
  7.1 0.0 copy-done.3
  7.1 0.0 copy-done.4
  7.1 1.5 %prepare.1 = (f32[8,128]{1,0:T(8,128)S(1)}, bf16[128,4096]{1,0:T(8,128)(2,1)S(1)}, bf16[128,4096]{1,0:T(8,128)(2,1)S(1)}, bf16[4096,256]{1,0:T(8,128)(2,1)S(1)}, f32[32,4096]{1,0:T(8,128)S(1)}) custom-call(s32[1,4]{1,0:T(1,128)S(1)} %bitcast.5, f32[1,128]{1,0:T(1,128)S(1)} %bitcast.6, f32[128,4096]{1,0:T(8,128)S(1)} %copy-done.1, ...), custom_call_target="tpu_custom_call" | custom-call | tf_op jit(solution)/shard_map/prepare/pallas_call | solution.py:376
  8.6 0.0 collective-permute-done.refs_0_
  8.6 0.3 %collective-permute-done.1.refs_1_ = f32[4,8,128]{2,1,0:T(8,128)S(1)} collective-permute-done((f32[4,8,128]{2,1,0:T(8,128)S(1)}, f32[4,8,128]{2,1,0:T(8,128)S(1)}, u32[]{:S(2)}, u32[]{:S(2)}) %collective-permute-start.1) | collective-permute-done | bytes 16416 | tf_op jit(solution)/shard_map/ppermute | solution.py:362
  8.9 1.3 %more.1.refs_0_ = f32[32,4096]{1,0:T(8,128)S(1)} custom-call(f32[8,128]{1,0:T(8,128)S(1)} %get-tuple-element.19.efficiency_ref, f32[4,16,4096]{2,1,0:T(8,128)S(1)} %copy-done, bf16[128,4096]{1,0:T(8,128)(2,1)S(1)} %get-tuple-element.20.high_ref, bf16[128,4096]{1,0:T(8,128)(2,1)S(1)} %get-tuple-element.21.low_ref, ...), custom_call_target="tpu_custom_call" | custom-call | tf_op jit(solution)/shard_map/more/pallas_call | solution.py:388
  10.2 1.3 %collective-permute-done.2.refs_1_ = f32[4,8,128]{2,1,0:T(8,128)S(1)} collective-permute-done((f32[4,8,128]{2,1,0:T(8,128)S(1)}, f32[4,8,128]{2,1,0:T(8,128)S(1)}, u32[]{:S(2)}, u32[]{:S(2)}) %collective-permute-start.2) | collective-permute-done | bytes 16416 | tf_op jit(solution)/shard_map/ppermute | solution.py:362
  11.4 1.2 %maps.1 = f32[16,1,128]{2,1,0:T(1,128)S(1)} custom-call(f32[8,128]{1,0:T(8,128)S(1)} %get-tuple-element.19.efficiency_ref, f32[4,16,4096]{2,1,0:T(8,128)S(1)} %copy-done, bf16[128,4096]{1,0:T(8,128)(2,1)S(1)} %get-tuple-element.20.high_ref, bf16[128,4096]{1,0:T(8,128)(2,1)S(1)} %get-tuple-element.21.low_ref, ...), custom_call_target="tpu_custom_call" | custom-call | tf_op jit(solution)/shard_map/maps/pallas_call | solution.py:400
  12.7 9.7 %all_to_all.5.got_ref = f32[16,1,128]{2,1,0:T(1,128)S(1)} all-to-all(f32[16,1,128]{2,1,0:T(1,128)S(1)} %maps.1), channel_id=1, replica_groups=mesh['cosmo'=2,'shell'=4,'band'=4] {'shell','band'}, dimensions={0} | all-to-all | bytes 16384 | tf_op jit(solution)/shard_map/all_to_all | solution.py:414
  22.4 0.8 %unpack.1 = f32[12,2,16]{2,1,0:T(2,128)} custom-call(f32[16,1,128]{2,1,0:T(1,128)S(1)} %all_to_all.5.got_ref), custom_call_target="tpu_custom_call" | custom-call | tf_op jit(solution)/shard_map/unpack/pallas_call | solution.py:415
  (1 shorter events, 0.0 us)
Async XLA Ops:
  0.9 6.2 %copy-start = (f32[4,16,4096]{2,1,0:T(8,128)S(1)}, f32[4,16,4096]{2,1,0:T(8,128)}, u32[]{:S(2)}) copy-start(f32[4,16,4096]{2,1,0:T(8,128)} %legendre_ref.5) | copy-start | bytes 3145732
  0.9 6.2 %copy-start.1 = (f32[128,4096]{1,0:T(8,128)S(1)}, f32[128,4096]{1,0:T(8,128)}, u32[]{:S(2)}) copy-start(f32[128,4096]{1,0:T(8,128)} %window_ref.1) | copy-start | bytes 6291460
  0.9 6.2 %copy-start.2 = (bf16[4,16,4096]{2,1,0:T(8,128)(2,1)S(1)}, bf16[4,16,4096]{2,1,0:T(8,128)(2,1)}, u32[]{:S(2)}) copy-start(bf16[4,16,4096]{2,1,0:T(8,128)(2,1)} %plus_ref.1) | copy-start | bytes 1572868
  0.9 6.2 %copy-start.3 = (bf16[4,16,4096]{2,1,0:T(8,128)(2,1)S(1)}, bf16[4,16,4096]{2,1,0:T(8,128)(2,1)}, u32[]{:S(2)}) copy-start(bf16[4,16,4096]{2,1,0:T(8,128)(2,1)} %minus_ref.1) | copy-start | bytes 1572868
  0.9 6.2 %copy-start.4 = (s32[4]{0:T(128)S(1)}, s32[4]{0:T(128)}, u32[]{:S(2)}) copy-start(s32[4]{0:T(128)} %param.15) | copy-start | bytes 52
  0.9 6.2 %copy-start.5 = (f32[128]{0:T(128)S(1)}, f32[128]{0:T(128)}, u32[]{:S(2)}) copy-start(f32[128]{0:T(128)} %param.14) | copy-start | bytes 1540
  1.0 7.6 %collective-permute-start = (f32[4,8,128]{2,1,0:T(8,128)S(1)}, f32[4,8,128]{2,1,0:T(8,128)S(1)}, u32[]{:S(2)}, u32[]{:S(2)}) collective-permute-start(f32[4,8,128]{2,1,0:T(8,128)S(1)} %get-tuple-element.24), channel_id=1, source_target_pairs={{0,2},{1,3},{2,1},{3,0},{4,6},{5,7},{6,5},{7,4},{8,10},{9,11},{10,... | collective-permute-start | bytes 49160 | tf_op jit(solution)/shard_map/ppermute | solution.py:362
  5.1 3.7 %collective-permute-start.1 = (f32[4,8,128]{2,1,0:T(8,128)S(1)}, f32[4,8,128]{2,1,0:T(8,128)S(1)}, u32[]{:S(2)}, u32[]{:S(2)}) collective-permute-start(f32[4,8,128]{2,1,0:T(8,128)S(1)} %get-tuple-element.25), channel_id=1, source_target_pairs={{0,1},{1,0},{2,3},{3,2},{4,5},{5,4},{6,7},{7,6},{8,9},{9,8},{10,11... | collective-permute-start | bytes 49160 | tf_op jit(solution)/shard_map/ppermute | solution.py:362
  6.7 4.7 %collective-permute-start.2 = (f32[4,8,128]{2,1,0:T(8,128)S(1)}, f32[4,8,128]{2,1,0:T(8,128)S(1)}, u32[]{:S(2)}, u32[]{:S(2)}) collective-permute-start(f32[4,8,128]{2,1,0:T(8,128)S(1)} %get-tuple-element.26), channel_id=1, source_target_pairs={{0,3},{1,2},{2,0},{3,1},{4,7},{5,6},{6,4},{7,5},{8,11},{9,10},{10,... | collective-permute-start | bytes 49160 | tf_op jit(solution)/shard_map/ppermute | solution.py:362
